TPU v7x, 64 devices: a 2x2x8 block of a 4x4x8 slice. The times are simulated.
64 devices in a mesh: dp: 4 (over x, y), tp: 16 (over z, core).
Axes of the slice: x: 2, y: 2, z: 8, core: 2. Of those that a mesh axis runs over, the one named last changes fastest.
The devices are a block of a 4x4x8 slice.
Arguments:
- x_steps: bfloat16 [3, 384, 6144], P(None, 'dp'), parts along dimension 1
- seq_lens: int32 [384], P(('dp', 'tp')), parts along dimension 0
- k_cache: bfloat16 [384, 3072, 128], P(('dp', 'tp')), parts along dimension 0
- v_cache: bfloat16 [384, 3072, 128], P(('dp', 'tp')), parts along dimension 0
- ln_gain: bfloat16 [6144], replicated
- ln_bias: bfloat16 [6144], replicated
- w_q: bfloat16 [6144, 6144], P(None, 'tp')
- b_q: bfloat16 [6144], P('tp')
- w_kv: bfloat16 [6144, 256], replicated
- b_kv: bfloat16 [256], replicated
- w_out: bfloat16 [6144, 6144], P('tp')
- b_out: bfloat16 [6144], replicated
Outputs:
- output 1: bfloat16 [3, 384, 6144], P(None, 'dp'), parts along dimension 1
- output 2: bfloat16 [384, 3072, 128], P(('dp', 'tp')), parts along dimension 0
- output 3: bfloat16 [384, 3072, 128], P(('dp', 'tp')), parts along dimension 0
There are 4 independent parts. A program takes and returns all parts, laid end to end along the dimension named above; an argument that names none is the same for every part.
All inputs are finite; a program needn't handle non-finite values.
Results may differ from a plain program's by a relative error of at most 0.0120439.
Values are sent between devices in bfloat16 or wider.
A program may use at most 768 MiB of HBM per device.

v0:
```python
import jax
import jax.numpy as jnp
from jax import lax
from jax.sharding import PartitionSpec as P

LN_EPS = 1e-5


def layer_norm(x_rows, ln_gain, ln_bias):
    x_float = x_rows.astype(jnp.float32)
    row_mean = jnp.mean(x_float, axis=-1, keepdims=True)
    centered = x_float - row_mean
    row_var = jnp.mean(centered * centered, axis=-1, keepdims=True)
    scaled = centered * lax.rsqrt(row_var + LN_EPS)
    return (scaled * ln_gain.astype(jnp.float32) + ln_bias.astype(jnp.float32)).astype(jnp.bfloat16)


def attend(q_rows, k_rows, v_rows, seq_lens, fresh_k, fresh_v):
    score_scale = q_rows.shape[-1] ** -0.5
    positions = jnp.arange(k_rows.shape[1], dtype=jnp.int32)
    old_scores = jnp.einsum('bhd,btd->bht', q_rows, k_rows, preferred_element_type=jnp.float32) * score_scale
    old_scores = jnp.where(positions[None, None, :] < seq_lens[:, None, None], old_scores, -jnp.inf)
    new_scores = jnp.einsum('bhd,bsd->bhs', q_rows, fresh_k, preferred_element_type=jnp.float32) * score_scale
    row_max = jnp.maximum(jnp.max(old_scores, axis=-1, keepdims=True), jnp.max(new_scores, axis=-1, keepdims=True))
    old_weights = jnp.exp(old_scores - row_max)
    new_weights = jnp.exp(new_scores - row_max)
    denominator = jnp.sum(old_weights, axis=-1, keepdims=True) + jnp.sum(new_weights, axis=-1, keepdims=True)
    numerator = jnp.einsum('bht,btd->bhd', old_weights.astype(jnp.bfloat16), v_rows, preferred_element_type=jnp.float32)
    numerator = numerator + jnp.einsum('bhs,bsd->bhd', new_weights.astype(jnp.bfloat16), fresh_v, preferred_element_type=jnp.float32)
    return (numerator / denominator).astype(jnp.bfloat16)


def write_cache(cache_rows, fresh_rows, seq_lens):
    offsets = jnp.arange(cache_rows.shape[1], dtype=jnp.int32)[None, :] - seq_lens[:, None]
    updated = cache_rows
    for slot_idx in range(fresh_rows.shape[1]):
        updated = jnp.where((offsets == slot_idx)[:, :, None], fresh_rows[:, slot_idx:slot_idx + 1, :], updated)
    return updated


def solution(mesh):
    tp_size = mesh.shape['tp']

    def local_block(x_steps, seq_lens, k_cache, v_cache, ln_gain, ln_bias, w_q, b_q, w_kv, b_kv, w_out, b_out):
        local_rows = k_cache.shape[0]
        head_dim = k_cache.shape[2]
        q_width = w_q.shape[1] * tp_size
        n_heads = q_width // head_dim
        row_start = lax.axis_index('tp') * local_rows
        fresh_keys = []
        fresh_values = []
        outputs = []
        for step_idx in range(x_steps.shape[0]):
            x_rows = x_steps[step_idx]
            normed = layer_norm(x_rows, ln_gain, ln_bias)
            q_part = (jnp.dot(normed, w_q, preferred_element_type=jnp.float32) + b_q.astype(jnp.float32)).astype(jnp.bfloat16)
            q_local = lax.all_to_all(q_part, 'tp', 0, 1, tiled=True)
            own_normed = lax.dynamic_slice_in_dim(normed, row_start, local_rows, axis=0)
            kv_rows = (jnp.dot(own_normed, w_kv, preferred_element_type=jnp.float32) + b_kv.astype(jnp.float32)).astype(jnp.bfloat16)
            fresh_keys.append(kv_rows[:, :head_dim])
            fresh_values.append(kv_rows[:, head_dim:])
            fresh_k = jnp.stack(fresh_keys, axis=1)
            fresh_v = jnp.stack(fresh_values, axis=1)
            attn_rows = attend(q_local.reshape(local_rows, n_heads, head_dim), k_cache, v_cache, seq_lens, fresh_k, fresh_v)
            attn_heads = lax.all_to_all(attn_rows.reshape(local_rows, q_width), 'tp', 1, 0, tiled=True)
            proj_part = jnp.dot(attn_heads, w_out, preferred_element_type=jnp.float32).astype(jnp.bfloat16)
            proj_sum = lax.psum(proj_part, 'tp')
            out_rows = x_rows.astype(jnp.float32) + proj_sum.astype(jnp.float32) + b_out.astype(jnp.float32)
            outputs.append(out_rows.astype(jnp.bfloat16))
        fresh_k = jnp.stack(fresh_keys, axis=1)
        fresh_v = jnp.stack(fresh_values, axis=1)
        return jnp.stack(outputs), write_cache(k_cache, fresh_k, seq_lens), write_cache(v_cache, fresh_v, seq_lens)

    row_spec = P(('dp', 'tp'), None, None)
    return jax.shard_map(
        local_block,
        mesh=mesh,
        in_specs=(P(None, 'dp', None), P(('dp', 'tp')), row_spec, row_spec, P(None), P(None), P(None, 'tp'), P('tp'), P(None, None), P(None), P('tp', None), P(None)),
        out_specs=(P(None, 'dp', None), row_spec, row_spec),
        check_vma=False,
    )
```

profile of v0, /device:TPU:21, one launch (start us, length us, event | category | flops | bytes accessed | tf_op | source)
XLA Modules:
  0.0 262.8 jit_solution(11776563079035352796)
XLA Ops:
  7.2 2.8 %convert_reduce_fusion.2 = (f32[96]{0:T(128)S(1)}, f32[96]{0:T(128)S(1)}, f32[96]{0:T(128)S(1)}) fusion(bf16[3,96,6144]{2,1,0:T(8,128)(2,1)} %param.12), kind=kLoop, calls=%fused_computation.29 | loop fusion | flops 3538656 | bytes 3540096 | tf_op jit(solution)/shard_map/reduce_sum | solution.py:11
  10.4 1.1 fusion.29
  11.6 3.0 %fusion.32 = (bf16[96,6144]{1,0:T(8,128)(2,1)}, bf16[96,6144]{1,0:T(8,128)(2,1)}, bf16[96,6144]{1,0:T(8,128)(2,1)S(1)}) fusion(f32[6144]{0:T(1024)S(1)} %convert_element_type.131, f32[6144]{0:T(1024)S(1)} %convert_element_type.130, f32[96]{0:T(128)S(1)} %add_rsqrt_fusion.2, f32[96]{0:T(128)S(1)} %broadcast_multiply_fusion.2, ...), kind=kLoop, calls=%fused_computation.50 | loop fusion | flops 10616832 | bytes 7129344 | tf_op jit(solution)/shard_map/convert_element_type | solution.py:15
  14.6 1.0 copy-done.4
  15.6 0.9 fusion.71
  16.5 0.7 all_to_all.92
  17.1 10.7 %all-to-all-start.4 = ((bf16[16,6,384]{2,1,0:T(8,128)(2,1)}), bf16[16,6,384]{2,1,0:T(8,128)(2,1)S(1)}, u32[]{:S(2)}, u32[]{:S(2)}) async-start(bf16[16,6,384]{2,1,0:T(8,128)(2,1)} %all_to_all.92), calls=%async_computation.4 | async-start | bytes 196608 | tf_op jit(solution)/shard_map/all_to_all | solution.py:57
  27.9 3.6 %fusion.69 = bf16[96,384]{1,0:T(8,128)(2,1)S(1)} fusion(bf16[96,6144]{1,0:T(8,128)(2,1)} %get-tuple-element.12, bf16[6144,384]{1,0:T(8,128)(2,1)} %param.18, f32[384]{0:T(512)S(1)} %convert_element_type.133), kind=kOutput, calls=%fused_computation.75 | convolution fusion | flops 453058560 | bytes 5973504 | tf_op jit(solution)/shard_map/dot_general | solution.py:56
  31.5 1.5 fusion.81
  33.6 3.3 %fusion.70 = bf16[96,384]{1,0:T(8,128)(2,1)S(1)} fusion(bf16[96,6144]{1,0:T(8,128)(2,1)S(1)} %copy-done.5, bf16[6144,384]{1,0:T(8,128)(2,1)} %param.18, f32[384]{0:T(512)S(1)} %convert_element_type.133), kind=kOutput, calls=%fused_computation.76 | convolution fusion | flops 453058560 | bytes 5973504 | tf_op jit(solution)/shard_map/dot_general | solution.py:56
  36.9 1.5 fusion.83
  38.3 0.8 fusion.86
  39.1 0.6 fusion.113
  39.7 0.6 fusion.114
  40.3 0.6 fusion.115
  40.9 0.6 pad_maximum_fusion.3
  41.5 0.7 all_to_all.85
  42.2 7.3 %all-to-all-start.2 = ((bf16[16,6,384]{2,1,0:T(8,128)(2,1)}), bf16[16,6,384]{2,1,0:T(8,128)(2,1)S(1)}, u32[]{:S(2)}, u32[]{:S(2)}) async-start(bf16[16,6,384]{2,1,0:T(8,128)(2,1)} %all_to_all.85), calls=%async_computation.2 | async-start | bytes 196608 | tf_op jit(solution)/shard_map/all_to_all | solution.py:57
  49.4 0.6 pad_maximum_fusion.4
  50.0 0.7 all_to_all.78
  50.7 6.6 %all-to-all-done.2 = bf16[16,6,384]{2,1,0:T(8,128)(2,1)S(1)} async-done(((bf16[16,6,384]{2,1,0:T(8,128)(2,1)}), bf16[16,6,384]{2,1,0:T(8,128)(2,1)S(1)}, u32[]{:S(2)}, u32[]{:S(2)}) %all-to-all-start.2) | async-done | bytes 73760 | tf_op jit(solution)/shard_map/all_to_all | solution.py:57
  57.4 3.8 %all-to-all-start = ((bf16[16,6,384]{2,1,0:T(8,128)(2,1)}), bf16[16,6,384]{2,1,0:T(8,128)(2,1)S(1)}, u32[]{:S(2)}, u32[]{:S(2)}) async-start(bf16[16,6,384]{2,1,0:T(8,128)(2,1)} %all_to_all.78), calls=%async_computation | async-start | bytes 196608 | tf_op jit(solution)/shard_map/all_to_all | solution.py:57
  61.5 5.9 %fusion.116 = (f32[6,48]{1,0:T(8,128)S(1)}, f32[6,48,3072]{2,1,0:T(8,128)}) fusion(bf16[6,48,128]{2,1,0:T(8,128)(2,1)S(1)} %reshape.223, bf16[6,3072,128]{2,1,0:T(8,128)(2,1)} %param.14, pred[6,3072]{1,0:T(8,128)(4,1)S(1)} %get-tuple-element.39), kind=kOutput, calls=%fused_computation.143 | convolution fusion | flops 229146336 | bytes 8350848 | tf_op jit(solution)/shard_map/bhd,btd->bht/dot_general | solution.py:21
  67.4 5.9 %fusion.118 = (f32[6,48]{1,0:T(8,128)S(1)}, f32[6,48,3072]{2,1,0:T(8,128)}) fusion(bf16[6,48,128]{2,1,0:T(8,128)(2,1)S(1)} %reshape.222, bf16[6,3072,128]{2,1,0:T(8,128)(2,1)} %param.14, pred[6,3072]{1,0:T(8,128)(4,1)S(1)} %get-tuple-element.39), kind=kOutput, calls=%fused_computation.145 | convolution fusion | flops 229146336 | bytes 8350848 | tf_op jit(solution)/shard_map/bhd,btd->bht/dot_general | solution.py:21
  73.5 4.2 %fusion.120 = (f32[6,48]{1,0:T(8,128)S(1)}, f32[6,48,3072]{2,1,0:T(8,128)S(1)}) fusion(bf16[6,48,128]{2,1,0:T(8,128)(2,1)S(1)} %reshape.221, bf16[6,3072,128]{2,1,0:T(8,128)(2,1)} %param.14, pred[6,3072]{1,0:T(8,128)(4,1)S(1)} %get-tuple-element.39), kind=kOutput, calls=%fused_computation.147 | convolution fusion | flops 229146336 | bytes 8350848 | tf_op jit(solution)/shard_map/bhd,btd->bht/dot_general | solution.py:21
  77.9 0.6 fusion.3
  78.5 3.4 %fusion.78 = bf16[6,48,128]{2,1,0:T(8,128)(2,1)S(1)} fusion(bf16[6,3072,128]{2,1,0:T(8,128)(2,1)} %param.15, f32[6,48,3072]{2,1,0:T(8,128)S(1)} %get-tuple-element.49, f32[6,48]{1,0:T(8,128)S(1)} %fusion.98, f32[6,48]{1,0:T(8,128)S(1)} %get-tuple-element.21, f32[6,128]{1,0:T(8,128)S(1)} %copy-done.8, f32[6,48]{1,0:T(8,128)S(1)} %get-tuple-element.20), kind=kOutput, calls=%fused_computation.80 | convolution fusion | flops 228409344 | bytes 8337792 | tf_op jit(solution)/shard_map/bht,btd->bhd/dot_general | solution.py:28
  82.0 0.7 copy.23
  82.6 7.2 %all-to-all-start.1 = ((bf16[6,16,384]{2,0,1:T(8,128)(2,1)}), bf16[6,16,384]{2,0,1:T(8,128)(2,1)S(1)}, u32[]{:S(2)}, u32[]{:S(2)}) async-start(bf16[6,16,384]{2,0,1:T(8,128)(2,1)} %copy.23), calls=%async_computation.1 | async-start | bytes 196608 | tf_op jit(solution)/shard_map/all_to_all | solution.py:65
  89.9 2.8 %fusion.5 = f32[6,48]{1,0:T(8,128)S(1)} fusion(f32[6,48,3072]{2,1,0:T(8,128)} %get-tuple-element.45, f32[6,48]{1,0:T(8,128)S(1)} %max.23), kind=kLoop, calls=%fused_computation.17 | loop fusion | flops 1769184 | bytes 3541248 | tf_op jit(solution)/shard_map/reduce_sum | solution.py:27
  92.9 3.4 %fusion.75 = bf16[6,48,128]{2,1,0:T(8,128)(2,1)S(1)} fusion(f32[6,48,128]{2,1,0:T(8,128)S(1)} %fusion.102, bf16[6,3072,128]{2,1,0:T(8,128)(2,1)} %param.15, f32[6,48,3072]{2,1,0:T(8,128)S(1)} %copy-done.3, f32[6,48]{1,0:T(8,128)S(1)} %max.23, f32[6,48]{1,0:T(8,128)S(1)} %add.173), kind=kOutput, calls=%fused_computation.79 | convolution fusion | flops 228372480 | bytes 8481024 | tf_op jit(solution)/shard_map/bht,btd->bhd/dot_general | solution.py:28
  96.4 0.7 copy.27
  97.1 2.6 fusion.7
  100.0 7.3 %all-to-all-start.3 = ((bf16[6,16,384]{2,0,1:T(8,128)(2,1)}), bf16[6,16,384]{2,0,1:T(8,128)(2,1)S(1)}, u32[]{:S(2)}, u32[]{:S(2)}) async-start(bf16[6,16,384]{2,0,1:T(8,128)(2,1)} %copy.27), calls=%async_computation.3 | async-start | bytes 196608 | tf_op jit(solution)/shard_map/all_to_all | solution.py:65
  107.2 5.1 %fusion.72 = bf16[6,48,128]{2,1,0:T(8,128)(2,1)} fusion(f32[6,48,128]{2,1,0:T(8,128)S(1)} %fusion.92, bf16[6,3072,128]{2,1,0:T(8,128)(2,1)} %param.15, f32[6,48,3072]{2,1,0:T(8,128)} %get-tuple-element.41, f32[6,48]{1,0:T(8,128)S(1)} %max.24, f32[6,48]{1,0:T(8,128)S(1)} %add.181), kind=kOutput, calls=%fused_computation.78 | convolution fusion | flops 228372480 | bytes 8481024 | tf_op jit(solution)/shard_map/bht,btd->bhd/dot_general | solution.py:28
  112.3 0.9 all_to_all.95
  113.2 0.7 copy.31
  113.9 0.7 all_to_all.84
  114.6 0.6 all-to-all-done.3
  115.2 6.7 %all-to-all-start.5 = ((bf16[6,16,384]{2,0,1:T(8,128)(2,1)}), bf16[6,16,384]{2,0,1:T(8,128)(2,1)S(1)}, u32[]{:S(2)}, u32[]{:S(2)}) async-start(bf16[6,16,384]{2,0,1:T(8,128)(2,1)} %copy.31), calls=%async_computation.5 | async-start | bytes 196608 | tf_op jit(solution)/shard_map/all_to_all | solution.py:65
  122.1 4.5 %convolution_convert_fusion.2 = bf16[96,6144]{1,0:T(8,128)(2,1)} fusion(bf16[96,384]{1,0:T(8,128)(2,1)} %all_to_all.84, bf16[384,6144]{1,0:T(8,128)(2,1)} %param.22), kind=kOutput, calls=%fused_computation.2 | convolution fusion | flops 453574656 | bytes 5971968 | tf_op jit(solution)/shard_map/dot_general | solution.py:66
  126.6 4.4 %convolution_convert_fusion.1 = bf16[96,6144]{1,0:T(8,128)(2,1)} fusion(bf16[96,384]{1,0:T(8,128)(2,1)S(1)} %all_to_all.91, bf16[384,6144]{1,0:T(8,128)(2,1)} %param.22), kind=kOutput, calls=%fused_computation.1 | convolution fusion | flops 453574656 | bytes 5971968 | tf_op jit(solution)/shard_map/dot_general | solution.py:66
  131.0 4.4 %convolution_convert_fusion = bf16[96,6144]{1,0:T(8,128)(2,1)} fusion(bf16[96,384]{1,0:T(8,128)(2,1)S(1)} %all_to_all.98, bf16[384,6144]{1,0:T(8,128)(2,1)} %param.22), kind=kOutput, calls=%fused_computation | convolution fusion | flops 453574656 | bytes 5971968 | tf_op jit(solution)/shard_map/dot_general | solution.py:66
  135.5 0.6 copy-done.12
  136.2 11.7 %select_select_fusion = (bf16[6,3072,128]{2,1,0:T(8,128)(2,1)}, bf16[6,3072,128]{2,1,0:T(8,128)(2,1)}) fusion(bf16[6,3072,128]{2,1,0:T(8,128)(2,1)} %param.15, pred[6,3072]{1,0:T(8,128)(4,1)S(1)} %copy-done.6, pred[6,3072]{1,0:T(8,128)(4,1)S(1)} %copy-done.7, pred[6,3072]{1,0:T(8,128)(4,1)S(1)} %get-tuple-element.36, bf16[6,128]{1,0:T(8,128)(2,1)S(1)} %copy-done.13, ...), kind=kLoop, calls=%fused_computation.3 | loop fusion | flops 14155776 | bytes 18938880 | tf_op jit(solution)/shard_map/jit(_where)/select_n | solution.py:37
  147.9 101.7 %all-reduce.3.cloned.1.call-done = (bf16[96,6144]{1,0:T(8,128)(2,1)}, bf16[96,6144]{1,0:T(8,128)(2,1)}, bf16[96,6144]{1,0:T(8,128)(2,1)}) async-done(((bf16[96,6144]{1,0:T(8,128)(2,1)}, bf16[96,6144]{1,0:T(8,128)(2,1)}, bf16[96,6144]{1,0:T(8,128)(2,1)}), (bf16[96,6144]{1,0:T(8,128)(2,1)}, bf16[96,6144]{1,0:T(8,128)(2,1)}, bf16[96,6144]{1,0:T(8,128)(2,1)})) %all-reduce.3.cloned.1.call-update) | async-done | bytes 3538960 | tf_op jit(solution)/shard_map/psum | solution.py:67
  249.6 4.3 %fusion.50 = (bf16[1,96,6144]{2,1,0:T(8,128)(2,1)S(1)}, bf16[1,96,6144]{2,1,0:T(8,128)(2,1)S(1)}, bf16[1,96,6144]{2,1,0:T(8,128)(2,1)S(1)}) fusion(bf16[96,6144]{1,0:T(8,128)(2,1)} %get-tuple-element.11, f32[6144]{0:T(1024)S(1)} %convert_element_type.142, bf16[3,96,6144]{2,1,0:T(8,128)(2,1)} %param.12, bf16[96,6144]{1,0:T(8,128)(2,1)} %get-tuple-element.10, ...), kind=kLoop, calls=%fused_computation.65 | loop fusion | flops 8847360 | bytes 10641408 | tf_op jit(solution)/shard_map/stack | solution.py:72
  253.9 2.0 pad_maximum_fusion
  (88 shorter events, 2.7 us)
Async XLA Ops:
  7.2 24.3 %copy-start = (bf16[6144,256]{1,0:T(8,128)(2,1)S(1)}, bf16[6144,256]{1,0:T(8,128)(2,1)}, u32[]{:S(2)}) copy-start(bf16[6144,256]{1,0:T(8,128)(2,1)} %param.20) | copy-start | bytes 9437188
  7.2 3.2 %copy-start.1 = (bf16[3,96,6144]{2,1,0:T(8,128)(2,1)S(1)}, bf16[3,96,6144]{2,1,0:T(8,128)(2,1)}, u32[]{:S(2)}) copy-start(bf16[3,96,6144]{2,1,0:T(8,128)(2,1)} %param.12) | copy-start | bytes 10616836
  7.2 4.3 %copy-start.21 = (bf16[384]{0:T(512)(128)(2,1)S(1)}, bf16[384]{0:T(512)(128)(2,1)}, u32[]{:S(2)}) copy-start(bf16[384]{0:T(512)(128)(2,1)} %param.19) | copy-start | bytes 2308
  7.2 4.3 %copy-start.10 = (bf16[6144]{0:T(1024)(128)(2,1)S(1)}, bf16[6144]{0:T(1024)(128)(2,1)}, u32[]{:S(2)}) copy-start(bf16[6144]{0:T(1024)(128)(2,1)} %param.16) | copy-start | bytes 36868
  7.2 4.3 %copy-start.11 = (bf16[6144]{0:T(1024)(128)(2,1)S(1)}, bf16[6144]{0:T(1024)(128)(2,1)}, u32[]{:S(2)}) copy-start(bf16[6144]{0:T(1024)(128)(2,1)} %param.17) | copy-start | bytes 36868
  11.6 4.0 %copy-start.2 = (bf16[6144,384]{1,0:T(8,128)(2,1)S(1)}, bf16[6144,384]{1,0:T(8,128)(2,1)}, u32[]{:S(2)}) copy-start(bf16[6144,384]{1,0:T(8,128)(2,1)} %param.18) | copy-start | bytes 14155780
  14.6 1.0 copy-start.4
  15.6 12.3 %copy-start.23 = (bf16[256]{0:T(256)(128)(2,1)S(1)}, bf16[256]{0:T(256)(128)(2,1)}, u32[]{:S(2)}) copy-start(bf16[256]{0:T(256)(128)(2,1)} %param.21) | copy-start | bytes 1540
  17.1 25.0 %all-to-all-start.4 = ((bf16[16,6,384]{2,1,0:T(8,128)(2,1)}), bf16[16,6,384]{2,1,0:T(8,128)(2,1)S(1)}, u32[]{:S(2)}, u32[]{:S(2)}) async-start(bf16[16,6,384]{2,1,0:T(8,128)(2,1)} %all_to_all.92), calls=%async_computation.4 | async-start | bytes 196608 | tf_op jit(solution)/shard_map/all_to_all | solution.py:57
  31.5 1.6 copy-start.5
  33.6 4.7 %copy-start.22 = (s32[6]{0:T(128)S(1)}, s32[6]{0:T(128)}, u32[]{:S(2)}) copy-start(s32[6]{0:T(128)} %param.13) | copy-start | bytes 76
  42.2 15.2 %all-to-all-start.2 = ((bf16[16,6,384]{2,1,0:T(8,128)(2,1)}), bf16[16,6,384]{2,1,0:T(8,128)(2,1)S(1)}, u32[]{:S(2)}, u32[]{:S(2)}) async-start(bf16[16,6,384]{2,1,0:T(8,128)(2,1)} %all_to_all.85), calls=%async_computation.2 | async-start | bytes 196608 | tf_op jit(solution)/shard_map/all_to_all | solution.py:57
  57.4 16.1 %all-to-all-start = ((bf16[16,6,384]{2,1,0:T(8,128)(2,1)}), bf16[16,6,384]{2,1,0:T(8,128)(2,1)S(1)}, u32[]{:S(2)}, u32[]{:S(2)}) async-start(bf16[16,6,384]{2,1,0:T(8,128)(2,1)} %all_to_all.78), calls=%async_computation | async-start | bytes 196608 | tf_op jit(solution)/shard_map/all_to_all | solution.py:57
  67.4 5.9 %copy-start.19 = (bf16[6,2,128]{2,0,1:T(8,128)(2,1)S(1)}, bf16[6,2,128]{2,0,1:T(8,128)(2,1)}, u32[]{:S(2)}) copy-start(bf16[6,2,128]{2,0,1:T(8,128)(2,1)} %pad_maximum_fusion.3) | copy-start | bytes 9220
  73.5 4.2 %copy-start.20 = (bf16[6,128,1]{1,0,2:T(8,128)(2,1)S(1)}, bf16[6,128,1]{1,0,2:T(8,128)(2,1)}, u32[]{:S(2)}) copy-start(bf16[6,128,1]{1,0,2:T(8,128)(2,1)} %get-tuple-element.31) | copy-start | bytes 4612
  77.7 0.8 copy-start.8
  81.9 10.7 %copy-start.9 = (bf16[6,2,128]{2,0,1:T(8,128)(2,1)S(1)}, bf16[6,2,128]{2,0,1:T(8,128)(2,1)}, u32[]{:S(2)}) copy-start(bf16[6,2,128]{2,0,1:T(8,128)(2,1)} %pad_maximum_fusion.4) | copy-start | bytes 9220
  82.6 17.3 %all-to-all-start.1 = ((bf16[6,16,384]{2,0,1:T(8,128)(2,1)}), bf16[6,16,384]{2,0,1:T(8,128)(2,1)S(1)}, u32[]{:S(2)}, u32[]{:S(2)}) async-start(bf16[6,16,384]{2,0,1:T(8,128)(2,1)} %copy.23), calls=%async_computation.1 | async-start | bytes 196608 | tf_op jit(solution)/shard_map/all_to_all | solution.py:65
  89.8 3.1 %copy-start.3 = (f32[6,48,3072]{2,1,0:T(8,128)S(1)}, f32[6,48,3072]{2,1,0:T(8,128)}, u32[]{:S(2)}) copy-start(f32[6,48,3072]{2,1,0:T(8,128)} %get-tuple-element.45) | copy-start | bytes 10616836
  100.0 15.2 %all-to-all-start.3 = ((bf16[6,16,384]{2,0,1:T(8,128)(2,1)}), bf16[6,16,384]{2,0,1:T(8,128)(2,1)S(1)}, u32[]{:S(2)}, u32[]{:S(2)}) async-start(bf16[6,16,384]{2,0,1:T(8,128)(2,1)} %copy.27), calls=%async_computation.3 | async-start | bytes 196608 | tf_op jit(solution)/shard_map/all_to_all | solution.py:65
  115.2 15.8 %all-to-all-start.5 = ((bf16[6,16,384]{2,0,1:T(8,128)(2,1)}), bf16[6,16,384]{2,0,1:T(8,128)(2,1)S(1)}, u32[]{:S(2)}, u32[]{:S(2)}) async-start(bf16[6,16,384]{2,0,1:T(8,128)(2,1)} %copy.31), calls=%async_computation.5 | async-start | bytes 196608 | tf_op jit(solution)/shard_map/all_to_all | solution.py:65
  121.8 127.8 %all-reduce.3.cloned.1.call-start = ((), (), s32[]{:S(2)}) async-start(), calls=%async_computation.6 | async-start | bytes 7077888 | tf_op jit(solution)/shard_map/psum | solution.py:67
  135.4 0.7 copy-start.12
  135.4 0.8 copy-start.6
  135.4 0.8 copy-start.7
  135.4 0.8 copy-start.13
  135.4 0.8 copy-start.14
  135.4 0.8 copy-start.15
  135.4 0.8 copy-start.16
  135.4 0.7 copy-start.17
  135.4 0.7 copy-start.18
Sparse Core Ops, SparseCore 0:
  135.6 113.9 all-reduce.2
where the time goes:
time: 264 us; the launch traced here: 263 us
  waiting for transfers between devices  109 us (41%)
  matrix products  53.3 us (20%)
  starting transfers between devices  43.2 us (16%)
  other arithmetic  33.6 us (13%)
  between operations  14.5 us (5%)
  local copies, waits for them, and re-layouts  9.18 us (3%)
    psum x1, waiting for transfers between devices, local_block(): proj_sum = lax.psum(proj_part, 'tp')  102 us
    all_to_all x3, starting transfers between devices, local_block(): q_local = lax.all_to_all(q_part, 'tp', 0, 1, tiled=True)  21.8 us
    all_to_all x3, starting transfers between devices, local_block(): lax.all_to_all(attn_rows.reshape(local_rows, q_width), 'tp', 1, 0, tiled=...  21.1 us
    dot_general x3, matrix products, attend(): jnp.einsum('bhd,btd->bht', q_rows, k_rows, preferred_element_type=jnp.flo...  16 us
    dot_general x3, matrix products, local_block(): jnp.dot(attn_heads, w_out, preferred_element_type=jnp.float32)  13.2 us
    dot_general x3, matrix products, attend(): jnp.einsum('bht,btd->bhd', old_weights.astype(jnp.bfloat16), v_rows, pref...  11.9 us
    select_n x1, other arithmetic, write_cache(): jnp.where((offsets == slot_idx)[:, :, None], fresh_rows[:, slot_idx:slot_...  11.7 us
    dot_general x3, matrix products, local_block(): jnp.dot(normed, w_q, preferred_element_type=jnp.float32)  7.75 us
  transfers between devices with their start and end apart: 7, of which 3 were waited for; matrix products, arithmetic and copies ran while one was open for 24% of the time, Pallas kernels for 0%

commit v1 on v0

v1 whole, which is shorter than its diff:
```python
import functools

import jax
import jax.numpy as jnp
from jax import lax
from jax.experimental import pallas as pl
from jax.experimental.pallas import tpu as pltpu
from jax.sharding import PartitionSpec as P

LN_EPS = 1e-5
LANES = 128
PACK = 16
VMEM_LIMIT = 60 * 1024 * 1024
MESH = pl.DeviceIdType.MESH
F32 = jnp.float32
BF16 = jnp.bfloat16


def iota(shape, dim):
    return lax.broadcasted_iota(jnp.int32, shape, dim)


def one_hot(cond):
    return jnp.where(cond, 1.0, 0.0).astype(BF16)


def mm(a, b):
    return jnp.dot(a, b, preferred_element_type=F32)


def peer(index):
    return {'tp': index}


def enter(me, n):
    barrier = pltpu.get_barrier_semaphore()
    for k in range(1, n):
        pl.semaphore_signal(barrier, inc=1, device_id=peer(lax.rem(me + k, n)), device_id_type=MESH)
    return barrier


def pack_rows(src, source_row, n, rows, send_buf):
    total, width = src.shape
    heads = width // LANES
    rest = rows - PACK
    shape = (n * PACK, total)
    dest = iota(shape, 0) // PACK
    slot = iota(shape, 0) % PACK
    col = iota(shape, 1)
    send_buf[:, :width] = mm(one_hot(col == source_row(dest, slot)), src).astype(BF16)
    extra = jnp.zeros((n * PACK, LANES), F32)
    hit = col == source_row(dest, PACK + slot % rest)
    for head in range(heads):
        extra += mm(one_hot(hit & (slot // rest == head)), src[:, head * LANES:(head + 1) * LANES])
    send_buf[:, width:] = extra.astype(BF16)


def unpack_rows(recv_buf, total, width, place, rows):
    heads = width // LANES
    rest = rows - PACK
    shape = (total, recv_buf.shape[0])
    source, slot = place(iota(shape, 0))
    col = iota(shape, 1)
    main = mm(one_hot((slot < PACK) & (col == source * PACK + slot)), recv_buf[:, :width])
    tail = recv_buf[:, width:]
    extra = [
        mm(one_hot((slot >= PACK) & (col == source * PACK + head * rest + slot - PACK)), tail)
        for head in range(heads)
    ]
    return (main + jnp.concatenate(extra, axis=1)).astype(BF16)


def exchange(me, n, send_buf, recv_buf, send_sem, recv_sem):
    mine = pl.ds(pl.multiple_of(me * PACK, PACK), PACK)
    copies = []
    order = sorted(range(1, n), key=lambda k: -min(k, n - k))
    for k in order:
        dest = lax.rem(me + k, n)
        copy = pltpu.make_async_remote_copy(
            src_ref=send_buf.at[pl.ds(pl.multiple_of(dest * PACK, PACK), PACK)],
            dst_ref=recv_buf.at[mine],
            send_sem=send_sem.at[k],
            recv_sem=recv_sem.at[k],
            device_id=peer(dest),
            device_id_type=MESH,
        )
        copy.start()
        copies.append(copy)
    recv_buf[mine] = send_buf[mine]
    return copies


def query_kernel(n, x_hbm, gain_ref, bias_ref, wq_hbm, bq_ref, wkv_hbm, bkv_ref, q_ref, kv_ref,
                 x_v, h_v, wq_v, wkv_v, acc, kv_acc, send_buf, recv_buf,
                 x_sem, wq_sem, wkv_sem, send_sem, recv_sem):
    me = lax.axis_index('tp')
    steps, group, width = x_v.shape
    q_cols = wq_v.shape[1]
    total = steps * group
    local = group // n
    rows = local * steps
    heads = q_cols // LANES
    barrier = enter(me, n)
    x_copies = []
    for s in range(steps):
        x_copies.append(pltpu.make_async_copy(x_hbm.at[s], x_v.at[s], x_sem.at[s]))
        x_copies[-1].start()
    wq_copy = pltpu.make_async_copy(wq_hbm, wq_v, wq_sem)
    wq_copy.start()
    wkv_copy = pltpu.make_async_copy(wkv_hbm, wkv_v, wkv_sem)
    wkv_copy.start()

    for s in range(steps):
        x_copies[s].wait()

        @pl.loop(0, group // PACK)
        def _(r):
            at = pl.ds(pl.multiple_of(r * PACK, PACK), PACK)
            x = x_v[s, at, :].astype(F32)
            mean = jnp.mean(x, axis=-1, keepdims=True)
            centered = x - mean
            var = jnp.mean(centered * centered, axis=-1, keepdims=True)
            scaled = centered * lax.rsqrt(var + LN_EPS)
            h = (scaled * gain_ref[...].astype(F32) + bias_ref[...].astype(F32)).astype(BF16)
            h_v[pl.ds(pl.multiple_of(s * group + r * PACK, PACK), PACK), :] = h

    depth = width // 8
    wq_copy.wait()
    acc[...] = jnp.zeros_like(acc)

    @pl.loop(0, width // depth)
    def _(c):
        at = pl.ds(pl.multiple_of(c * depth, depth), depth)
        acc[...] += mm(h_v[:, at], wq_v[at, :])

    q = (acc[...] + bq_ref[...].astype(F32)).astype(BF16)
    pack_rows(q, lambda dest, r: (r % steps) * group + dest * local + r // steps, n, rows, send_buf)
    pl.semaphore_wait(barrier, n - 1)
    copies = exchange(me, n, send_buf, recv_buf, send_sem, recv_sem)

    wkv_copy.wait()
    kv_acc[...] = jnp.zeros_like(kv_acc)

    @pl.loop(0, width // depth)
    def _(c):
        at = pl.ds(pl.multiple_of(c * depth, depth), depth)
        kv_acc[...] += mm(h_v[:, at], wkv_v[at, :])

    kv = (kv_acc[...] + bkv_ref[...].astype(F32)).astype(BF16)
    pad = kv_ref.shape[1]
    shape = (local * pad, total)
    row = iota(shape, 0)
    own = one_hot((row % pad < steps) & (iota(shape, 1) == (row % pad) * group + me * local + row // pad))
    kv_ref[...] = mm(own, kv).astype(F32).reshape(kv_ref.shape)

    for copy in copies:
        copy.wait()
    per_seq = n * steps
    q_all = unpack_rows(
        recv_buf, total, q_cols,
        lambda row: ((row % per_seq) // steps, (row // per_seq) * steps + row % steps), rows)
    for i in range(local):
        for head in range(heads):
            q_ref[i, head * per_seq:(head + 1) * per_seq, :] = q_all[
                i * per_seq:(i + 1) * per_seq, head * LANES:(head + 1) * LANES]


def attend_kernel(steps, block, lens_ref, q_ref, kv_ref, k_ref, v_ref, o_ref, ko_ref, vo_ref, scores):
    seq_len = lens_ref[pl.program_id(0)]
    n_rows, head_dim = q_ref.shape[1:]
    cache_len = k_ref.shape[1]
    window = 2 * PACK
    ko_ref[...] = k_ref[...]
    vo_ref[...] = v_ref[...]
    start = jnp.minimum((seq_len // PACK) * PACK, cache_len - window)
    at = pl.ds(pl.multiple_of(start, PACK), window)
    pos = iota((window, head_dim), 0) + start
    k_win = ko_ref[0, at, :].astype(F32)
    v_win = vo_ref[0, at, :].astype(F32)
    for s in range(steps):
        k_win = jnp.where(pos == seq_len + s, kv_ref[0, s:s + 1, :head_dim], k_win)
        v_win = jnp.where(pos == seq_len + s, kv_ref[0, s:s + 1, head_dim:], v_win)
    ko_ref[0, at, :] = k_win.astype(BF16)
    vo_ref[0, at, :] = v_win.astype(BF16)

    n_blocks = (seq_len + steps + block - 1) // block
    factor = head_dim ** -0.5 * 1.4426950408889634
    last = seq_len + iota((n_rows, block), 0) % steps
    col = iota((n_rows, block), 1)
    q = q_ref[0]

    def fold(value, op):
        out = value[:, :LANES]
        for c in range(1, block // LANES):
            out = op(out, value[:, c * LANES:(c + 1) * LANES])
        return out

    def first(j, top):
        at = pl.ds(pl.multiple_of(j * block, block), block)
        t = lax.dot_general(q, ko_ref[0, at, :], (((1,), (1,)), ((), ())), preferred_element_type=F32)
        t = jnp.where(col <= last - j * block, t, -jnp.inf)
        scores[:, at] = t
        return jnp.maximum(top, fold(t, jnp.maximum))

    top = lax.fori_loop(0, n_blocks, first, jnp.full((n_rows, LANES), -jnp.inf, F32))
    top = jnp.max(top, axis=-1, keepdims=True)

    def second(j, carry):
        den, num = carry
        at = pl.ds(pl.multiple_of(j * block, block), block)
        p = jnp.exp2((scores[:, at] - top) * factor)
        num = num + mm(p.astype(BF16), vo_ref[0, at, :])
        return den + fold(p, jnp.add), num

    zero = jnp.zeros((n_rows, LANES), F32)
    den, num = lax.fori_loop(0, n_blocks, second, (zero, zero))
    out = (num / jnp.sum(den, axis=-1, keepdims=True)).astype(BF16)
    per_seq = o_ref.shape[1]
    for head in range(n_rows // per_seq):
        o_ref[0, :, head * LANES:(head + 1) * LANES] = out[head * per_seq:(head + 1) * per_seq]


def project_kernel(n, steps, o_ref, x_hbm, wo_hbm, bo_hbm, y_hbm,
                   a_v, wo_v, x_v, bo_v, part, pair_send, pair_recv, rs_send, rs_recv, y_v, send_buf, recv_buf,
                   wo_sem, in_sem, a_send, a_recv, pair_ssem, pair_rsem, rs_ssem, rs_rsem, ag_ssem, ag_rsem,
                   d2d_ssem, d2d_rsem, out_sem):
    me = lax.axis_index('tp')
    total, depth = a_v.shape
    cols = wo_v.shape[2]
    chips = n // 2
    far = chips // 2
    chip = me // 2
    core = me % 2
    mate = me + 1 - 2 * core
    group = total // steps
    local = group // n
    rows = local * steps
    per_seq = n * steps
    half = total // 2
    barrier = enter(me, n)

    def block_at(index):
        return pl.ds(pl.multiple_of(index * cols, LANES), cols)

    def half_at(h):
        return pl.ds(h * half, half)

    offsets = [far]
    for k in range(far - 1, 0, -1):
        offsets += [k, chips - k]
    offsets.append(0)
    wo_copies = []
    for pos, off in enumerate(offsets):
        dest = lax.rem(chip + off, chips)
        for side, dev in enumerate((2 * dest + 1 - core, 2 * dest + core)):
            copy = pltpu.make_async_copy(wo_hbm.at[:, block_at(dev)], wo_v.at[2 * pos + side], wo_sem.at[2 * pos + side])
            copy.start()
            wo_copies.append(copy)
    x_copy = pltpu.make_async_copy(x_hbm.at[:, block_at(me)], x_v, in_sem.at[0])
    x_copy.start()
    bo_copy = pltpu.make_async_copy(bo_hbm.at[:, block_at(me)], bo_v, in_sem.at[1])
    bo_copy.start()

    pack_rows(o_ref[...], lambda dest, r: (r // steps) * per_seq + dest * steps + r % steps, n, rows, send_buf)
    pl.semaphore_wait(barrier, n - 1)
    copies = exchange(me, n, send_buf, recv_buf, a_send, a_recv)
    for copy in copies:
        copy.wait()
    a_v[...] = unpack_rows(
        recv_buf, total, depth,
        lambda row: ((row % group) // local, (row % local) * steps + row // group), rows)

    pair_copies = {}

    def multiply(off):
        pos = offsets.index(off)
        wo_copies[2 * pos].wait()
        pair_send[pos] = mm(a_v[...], wo_v[2 * pos]).astype(BF16)
        copy = pltpu.make_async_remote_copy(
            src_ref=pair_send.at[pos], dst_ref=pair_recv.at[pos], send_sem=pair_ssem.at[pos],
            recv_sem=pair_rsem.at[pos], device_id=peer(mate), device_id_type=MESH)
        copy.start()
        pair_copies[off] = copy
        wo_copies[2 * pos + 1].wait()
        part[pos] = mm(a_v[...], wo_v[2 * pos + 1])

    arrived = set()

    def chip_sum(off, h):
        pos = offsets.index(off)
        if off not in arrived:
            pair_copies[off].wait_recv()
            arrived.add(off)
        return part[pos, half_at(h), :] + pair_recv[pos, half_at(h), :].astype(F32)

    sign = (-1, 1)
    plan = [[(far, d)] + [(k, h) for k in range(far - 1, 0, -1) for h in (1 - d, d)] for d in (0, 1)]
    n_slots = len(plan[0])
    nexts = [2 * lax.rem(chip + chips + sign[d], chips) + core for d in (0, 1)]
    rs_copies = [[], []]

    def reduce_slot(d, slot):
        k, h = plan[d][slot]
        value = chip_sum((sign[d] * k) % chips, h)
        if slot >= 2:
            rs_copies[d][slot - 2].wait_recv()
            value = value + rs_recv[d, slot - 2].astype(F32)
        rs_send[d, slot] = value.astype(BF16)
        copy = pltpu.make_async_remote_copy(
            src_ref=rs_send.at[d, slot], dst_ref=rs_recv.at[d, slot], send_sem=rs_ssem.at[d, slot],
            recv_sem=rs_rsem.at[d, slot], device_id=peer(nexts[d]), device_id_type=MESH)
        copy.start()
        rs_copies[d].append(copy)

    todo = list(offsets)
    multiply(todo.pop(0))
    multiply(todo.pop(0))
    for slot in range(n_slots):
        for d in (0, 1):
            need = (sign[d] * plan[d][slot][0]) % chips
            while need in todo:
                multiply(todo.pop(0))
            reduce_slot(d, slot)
        for _ in range(2):
            if todo:
                multiply(todo.pop(0))

    x_copy.wait()
    bo_copy.wait()
    for d in (0, 1):
        rs_copies[d][n_slots - 2].wait_recv()
        rs_copies[d][n_slots - 1].wait_recv()
    own = 2 * chip + core
    for h in (0, 1):
        value = chip_sum(0, h)
        for d in (0, 1):
            slot = n_slots - 1 if h == d else n_slots - 2
            value = value + rs_recv[d, slot].astype(F32)
        value = x_v[half_at(h), :].astype(F32) + value + bo_v[...].astype(F32)
        y_v[own, half_at(h), :] = value.astype(BF16)

    d2d_copies = []
    out_copies = []

    def spread(index, hop, h):
        at = y_v.at[index, half_at(h)]
        pos = 2 * hop + h
        copy = pltpu.make_async_remote_copy(
            src_ref=at, dst_ref=at, send_sem=d2d_ssem.at[pos], recv_sem=d2d_rsem.at[pos],
            device_id=peer(mate), device_id_type=MESH)
        copy.start()
        other = index + 1 - 2 * core
        d2d_copies.append((copy, other, h, pos))
        out = pltpu.make_async_copy(at, y_hbm.at[half_at(h), block_at(index)], out_sem.at[0, pos])
        out.start()
        out_copies.append(out)

    ag_copies = [[], []]

    def gather_slot(d, slot, index, h):
        at = y_v.at[index, half_at(h)]
        copy = pltpu.make_async_remote_copy(
            src_ref=at, dst_ref=at, send_sem=ag_ssem.at[d, slot], recv_sem=ag_rsem.at[d, slot],
            device_id=peer(nexts[d]), device_id_type=MESH)
        copy.start()
        ag_copies[d].append(copy)

    for j in (0, 1):
        for d in (0, 1):
            gather_slot(d, j, own, 1 - d if j == 0 else d)
    for h in (0, 1):
        spread(own, 0, h)
    for slot in range(n_slots):
        back = slot // 2 + 1
        for d in (0, 1):
            h = 1 - d if slot % 2 == 0 else d
            hop = (-sign[d] * back) % chips
            index = 2 * lax.rem(chip + hop, chips) + core
            ag_copies[d][slot].wait_recv()
            if slot + 2 < n_slots:
                gather_slot(d, slot + 2, index, h)
            spread(index, hop, h)
    for copy, other, h, pos in d2d_copies:
        copy.wait_recv()
        out = pltpu.make_async_copy(
            y_v.at[other, half_at(h)], y_hbm.at[half_at(h), block_at(other)], out_sem.at[1, pos])
        out.start()
        out_copies.append(out)
    for copy in pair_copies.values():
        copy.wait_send()
    for d in (0, 1):
        for copy in rs_copies[d] + ag_copies[d]:
            copy.wait_send()
    for copy, _, _, _ in d2d_copies:
        copy.wait_send()
    for out in out_copies:
        out.wait()


def solution(mesh):
    n = mesh.shape['tp']
    vmem = pl.BlockSpec(memory_space=pltpu.VMEM)
    anywhere = pl.BlockSpec(memory_space=pl.ANY)
    dma = pltpu.SemaphoreType.DMA

    def local_block(x_steps, seq_lens, k_cache, v_cache, ln_gain, ln_bias, w_q, b_q, w_kv, b_kv, w_out, b_out):
        steps, group, width = x_steps.shape
        local, cache_len, head_dim = k_cache.shape
        total = steps * group
        q_cols = w_q.shape[1]
        kv_cols = w_kv.shape[1]
        heads = q_cols // head_dim
        per_seq = n * steps
        pad = 8
        q_rows, kv_rows = pl.pallas_call(
            functools.partial(query_kernel, n),
            name='query',
            out_shape=(
                jax.ShapeDtypeStruct((local, heads * per_seq, head_dim), BF16),
                jax.ShapeDtypeStruct((local, pad, kv_cols), F32),
            ),
            in_specs=[anywhere, vmem, vmem, anywhere, vmem, anywhere, vmem],
            out_specs=(vmem, vmem),
            scratch_shapes=[
                pltpu.VMEM((steps, group, width), BF16),
                pltpu.VMEM((total, width), BF16),
                pltpu.VMEM((width, q_cols), BF16),
                pltpu.VMEM((width, kv_cols), BF16),
                pltpu.VMEM((total, q_cols), F32),
                pltpu.VMEM((total, kv_cols), F32),
                pltpu.VMEM((n * PACK, q_cols + LANES), BF16),
                pltpu.VMEM((n * PACK, q_cols + LANES), BF16),
                dma((steps,)), dma, dma, dma((n,)), dma((n,)),
            ],
            compiler_params=pltpu.CompilerParams(
                collective_id=0, has_side_effects=True, vmem_limit_bytes=VMEM_LIMIT),
        )(x_steps, ln_gain[None], ln_bias[None], w_q, b_q[None], w_kv, b_kv[None])

        block = cache_len // 3 if cache_len % (3 * LANES) == 0 else cache_len
        per_row = lambda i, lens: (i, 0, 0)
        out_heads, k_out, v_out = pl.pallas_call(
            functools.partial(attend_kernel, steps, block),
            name='attend',
            out_shape=(
                jax.ShapeDtypeStruct((local, per_seq, q_cols), BF16),
                jax.ShapeDtypeStruct(k_cache.shape, BF16),
                jax.ShapeDtypeStruct(v_cache.shape, BF16),
            ),
            grid_spec=pltpu.PrefetchScalarGridSpec(
                num_scalar_prefetch=1,
                grid=(local,),
                in_specs=[
                    pl.BlockSpec((1, heads * per_seq, head_dim), per_row),
                    pl.BlockSpec((1, pad, kv_cols), per_row),
                    pl.BlockSpec((1, cache_len, head_dim), per_row),
                    pl.BlockSpec((1, cache_len, head_dim), per_row),
                ],
                out_specs=(
                    pl.BlockSpec((1, per_seq, q_cols), per_row),
                    pl.BlockSpec((1, cache_len, head_dim), per_row),
                    pl.BlockSpec((1, cache_len, head_dim), per_row),
                ),
                scratch_shapes=[pltpu.VMEM((heads * per_seq, cache_len), F32)],
            ),
            compiler_params=pltpu.CompilerParams(vmem_limit_bytes=VMEM_LIMIT),
        )(seq_lens, q_rows, kv_rows, k_cache, v_cache)

        cols = width // n
        chips = n // 2
        n_slots = chips - 1
        half = total // 2
        y = pl.pallas_call(
            functools.partial(project_kernel, n, steps),
            name='project',
            out_shape=jax.ShapeDtypeStruct((total, width), BF16),
            in_specs=[vmem, anywhere, anywhere, anywhere],
            out_specs=anywhere,
            scratch_shapes=[
                pltpu.VMEM((total, q_cols), BF16),
                pltpu.VMEM((n, q_cols, cols), BF16),
                pltpu.VMEM((total, cols), BF16),
                pltpu.VMEM((1, cols), BF16),
                pltpu.VMEM((chips, total, cols), F32),
                pltpu.VMEM((chips, total, cols), BF16),
                pltpu.VMEM((chips, total, cols), BF16),
                pltpu.VMEM((2, n_slots, half, cols), BF16),
                pltpu.VMEM((2, n_slots, half, cols), BF16),
                pltpu.VMEM((n, total, cols), BF16),
                pltpu.VMEM((n * PACK, q_cols + LANES), BF16),
                pltpu.VMEM((n * PACK, q_cols + LANES), BF16),
                dma((n,)), dma((2,)), dma((n,)), dma((n,)), dma((chips,)), dma((chips,)),
                dma((2, n_slots)), dma((2, n_slots)), dma((2, n_slots)), dma((2, n_slots)),
                dma((2 * chips,)), dma((2 * chips,)), dma((2, 2 * chips)),
            ],
            compiler_params=pltpu.CompilerParams(
                collective_id=1, has_side_effects=True, vmem_limit_bytes=VMEM_LIMIT),
        )(out_heads.reshape(total, q_cols), x_steps.reshape(total, width), w_out, b_out[None])
        return y.reshape(x_steps.shape), k_out, v_out

    row_spec = P(('dp', 'tp'), None, None)
    return jax.shard_map(
        local_block,
        mesh=mesh,
        in_specs=(P(None, 'dp', None), P(('dp', 'tp')), row_spec, row_spec, P(None), P(None), P(None, 'tp'), P('tp'), P(None, None), P(None), P('tp', None), P(None)),
        out_specs=(P(None, 'dp', None), row_spec, row_spec),
        check_vma=False,
    )
```

time: 264 us -> 111 us (0.42)
  waiting for transfers between devices: 109 us -> 0 us
  Pallas kernels: 0 us -> 99.1 us
  matrix products: 53.3 us -> 0 us
  starting transfers between devices: 43.2 us -> 0 us
  other arithmetic: 33.6 us -> 0 us
  between operations: 14.5 us -> 0.65 us
    psum x1 -> x0, waiting for transfers between devices: 102 us -> none  [local_block(): proj_sum = lax.psum(proj_part, 'tp')]
    pallas_call x0 -> x3, Pallas kernels: none -> 99.1 us  [the longest x1 58.2 us: local_block(): pl.pallas_call(functools.partial(project_kernel, n, steps), name='project...]
    dot_general x20 -> x0, matrix products: 53.3 us -> none  [the longest x3 16 us: attend(): jnp.einsum('bhd,btd->bht', q_rows, k_rows, preferred_element_type=jnp.flo...]
    all_to_all x6 -> x0, starting transfers between devices: 42.9 us -> none  [the longest x3 21.8 us: local_block(): q_local = lax.all_to_all(q_part, 'tp', 0, 1, tiled=True)]
    select_n x1 -> x0, other arithmetic: 11.7 us -> none  [write_cache(): jnp.where((offsets == slot_idx)[:, :, None], fresh_rows[:, slot_idx:slot_...]
    reduce_sum x7 -> x0, other arithmetic: 9.95 us -> none  [the longest x3 6.02 us: attend(): jnp.sum(old_weights, axis=-1, keepdims=True)]
    another operation x7 -> x0, other arithmetic: 7.51 us -> none  [the longest x2 6.3 us: local_block(): jnp.stack(outputs)]
    all_to_all x6 -> x0, waiting for transfers between devices: 7.2 us -> none  [the longest x3 6.61 us: local_block(): q_local = lax.all_to_all(q_part, 'tp', 0, 1, tiled=True)]
  transfers between devices with their start and end apart: 7 -> 0, of which waited for: 3 -> 0; matrix products, arithmetic and copies ran while one was open for 24% -> 0% of each run, Pallas kernels for 0% -> 0%
where the time goes in v1:
time: 111 us; the launch traced here: 110 us
  Pallas kernels  99.1 us (89%)
  local copies, waits for them, and re-layouts  10.6 us (10%)
    pallas_call x1, Pallas kernels, local_block(): pl.pallas_call(functools.partial(project_kernel, n, steps), name='project...  58.2 us
    pallas_call x1, Pallas kernels, local_block(): pl.pallas_call(functools.partial(query_kernel, n), name='query', out_shap...  28.4 us
    pallas_call x1, Pallas kernels, local_block(): pl.pallas_call(functools.partial(attend_kernel, steps, block), name='atte...  12.5 us
    unnamed x1, local copies, waits for them, and re-layouts  4.17 us

profile of v1, /device:TPU:21, one launch (start us, length us, event | category | flops | bytes accessed | tf_op | source)
XLA Modules:
  0.0 110.4 jit_solution(15769847438166793690)
XLA Ops:
  0.6 1.2 %broadcast_in_dim.18.bkv_ref = bf16[1,256]{1,0:T(2,128)(2,1)} reshape(bf16[256]{0:T(256)(128)(2,1)} %param.21) | data formatting | bytes 1024 | tf_op jit(solution)/shard_map/broadcast_in_dim | solution.py:437
  1.9 1.2 %broadcast_in_dim.17.bq_ref = bf16[1,384]{1,0:T(2,128)(2,1)} reshape(bf16[384]{0:T(512)(128)(2,1)} %param.19) | data formatting | bytes 1536 | tf_op jit(solution)/shard_map/broadcast_in_dim | solution.py:437
  3.1 1.3 %broadcast_in_dim.15.gain_ref = bf16[1,6144]{1,0:T(2,128)(2,1)} reshape(bf16[6144]{0:T(1024)(128)(2,1)} %param.16) | data formatting | bytes 24576 | tf_op jit(solution)/shard_map/broadcast_in_dim | solution.py:437
  4.4 1.3 %broadcast_in_dim.16.bias_ref = bf16[1,6144]{1,0:T(2,128)(2,1)} reshape(bf16[6144]{0:T(1024)(128)(2,1)} %param.17) | data formatting | bytes 24576 | tf_op jit(solution)/shard_map/broadcast_in_dim | solution.py:437
  5.8 1.3 %broadcast_in_dim.19.bo_hbm = bf16[1,6144]{1,0:T(2,128)(2,1)} reshape(bf16[6144]{0:T(1024)(128)(2,1)} %param.23) | data formatting | bytes 24576 | tf_op jit(solution)/shard_map/broadcast_in_dim | solution.py:497
  7.1 28.4 %query.1 = (bf16[6,144,128]{2,1,0:T(8,128)(2,1)}, f32[6,8,256]{2,1,0:T(8,128)}) custom-call(bf16[3,96,6144]{2,1,0:T(8,128)(2,1)} %x_hbm.1, bf16[1,6144]{1,0:T(2,128)(2,1)} %broadcast_in_dim.15.gain_ref, bf16[1,6144]{1,0:T(2,128)(2,1)} %broadcast_in_dim.16.bias_ref, bf16[6144,384]{1,0:T(8,128)(2,1)} %wq_hbm.1, bf16[1,384]{1,0:T(2,128)(2,1)} %broadcast_in_dim.17.bq_ref, ...), custom_call_target="tpu_custom_call" | custom-call | tf_op jit(solution)/shard_map/query/pallas_call | solution.py:415
  35.5 12.5 %attend.1 = (bf16[6,48,384]{2,1,0:T(8,128)(2,1)}, bf16[6,3072,128]{2,1,0:T(8,128)(2,1)}, bf16[6,3072,128]{2,1,0:T(8,128)(2,1)}) custom-call(s32[6]{0:T(128)} %lens_ref.1, bf16[6,144,128]{2,1,0:T(8,128)(2,1)} %get-tuple-element.8.q_ref, f32[6,8,256]{2,1,0:T(8,128)} %get-tuple-element.9.kv_ref, bf16[6,3072,128]{2,1,0:T(8,128)(2,1)} %k_ref.1, ...), custom_call_target="tpu_custom_call" | custom-call | tf_op jit(solution)/shard_map/attend/pallas_call | solution.py:441
  48.0 58.2 %project.1 = bf16[288,6144]{1,0:T(8,128)(2,1)} custom-call(bf16[288,384]{1,0:T(8,128)(2,1)} %bitcast.5, bf16[288,6144]{1,0:T(8,128)(2,1)} %bitcast.3, bf16[384,6144]{1,0:T(8,128)(2,1)} %wo_hbm.1, bf16[1,6144]{1,0:T(2,128)(2,1)} %broadcast_in_dim.19.bo_hbm), custom_call_target="tpu_custom_call" | custom-call | tf_op jit(solution)/shard_map/project/pallas_call | solution.py:472
  106.2 4.2 %copy.16 = bf16[3,96,6144]{2,1,0:T(8,128)(2,1)} copy(bf16[3,96,6144]{2,1,0:T(8,128)(2,1)} %bitcast.4) | data formatting | bytes 7077888

commit v2 on v0

v2 whole, which is shorter than its diff:
```python
import functools

import jax
import jax.numpy as jnp
from jax import lax
from jax.experimental import pallas as pl
from jax.experimental.pallas import tpu as pltpu
from jax.sharding import PartitionSpec as P

LN_EPS = 1e-5
LANES = 128
PACK = 16
PARTS = 2
VMEM_LIMIT = 60 * 1024 * 1024
MESH = pl.DeviceIdType.MESH
F32 = jnp.float32
BF16 = jnp.bfloat16


def iota(shape, dim):
    return lax.broadcasted_iota(jnp.int32, shape, dim)


def one_hot(rows, cols, index, valid=None):
    at = index if valid is None else jnp.where(valid, index, -1)
    return jnp.where(iota((rows, cols), 1) == at, 1.0, 0.0).astype(BF16)


def mm(a, b):
    return jnp.dot(a, b, preferred_element_type=F32)


def peer(index):
    return {'tp': index}


def tiles_of(head, rows):
    return range(head * rows // PACK, ((head + 1) * rows - 1) // PACK + 1)


def pack_rows(src, source_row, n, rows, send_buf):
    total, width = src.shape
    heads = width // LANES
    p = iota((n * PACK, 1), 0)
    dest, slot = p // PACK, p % PACK
    for tile in range(send_buf.shape[-1] // LANES):
        unit = tile * PACK + slot
        index = source_row(dest, unit % rows)
        value = jnp.zeros((n * PACK, LANES), F32)
        for head in range(heads):
            if tile in tiles_of(head, rows):
                hot = one_hot(n * PACK, total, index, unit // rows == head)
                value += mm(hot, src[:, head * LANES:(head + 1) * LANES])
        send_buf[:, tile * LANES:(tile + 1) * LANES] = value.astype(BF16)


def unpack_rows(recv_buf, total, heads, place, rows):
    source, row = place(iota((total, 1), 0))
    out = []
    for head in range(heads):
        unit = head * rows + row
        value = jnp.zeros((total, LANES), F32)
        for tile in tiles_of(head, rows):
            hot = one_hot(total, recv_buf.shape[0], source * PACK + unit % PACK, unit // PACK == tile)
            value += mm(hot, recv_buf[:, tile * LANES:(tile + 1) * LANES])
        out.append(value.astype(BF16))
    return out


def spread_row(row_ref, src_ref):
    for j in range(src_ref.shape[0]):
        row_ref[:, j * LANES:(j + 1) * LANES] = src_ref[j:j + 1, :].astype(F32)


def local_kernel(n, lens_ref, x_hbm, gain_ref, bias_ref, wq_hbm, bq_ref, wkv_hbm, bkv_ref, k_hbm, v_hbm,
                 pieces_ref, ko_hbm, vo_hbm,
                 x_v, h_v, wq_v, wkv_v, k_v, v_v, acc, kv_acc, gain_v, bias_v, bq_v, bkv_v, fresh,
                 x_sem, w_sem, in_sem, out_sem):
    me = lax.axis_index('tp')
    steps, group, width = x_v.shape
    q_cols = wq_v.shape[1]
    total = steps * group
    local, cache_len, head_dim = k_v.shape
    x_copies = [pltpu.make_async_copy(x_hbm.at[s], x_v.at[s], x_sem.at[s]) for s in range(steps)]
    wkv_copy = pltpu.make_async_copy(wkv_hbm, wkv_v, w_sem.at[0])
    wq_copy = pltpu.make_async_copy(wq_hbm, wq_v, w_sem.at[1])
    caches = ((k_hbm, k_v, ko_hbm), (v_hbm, v_v, vo_hbm))
    ins = [[pltpu.make_async_copy(src.at[i], mid.at[i], in_sem.at[c, i]) for i in range(local)]
           for c, (src, mid, _) in enumerate(caches)]
    outs = [[pltpu.make_async_copy(mid.at[i], dst.at[i], out_sem.at[c, i]) for i in range(local)]
            for c, (_, mid, dst) in enumerate(caches)]
    for copy in x_copies + [wkv_copy] + ins[0] + ins[1] + [wq_copy]:
        copy.start()
    spread_row(gain_v, gain_ref)
    spread_row(bias_v, bias_ref)
    spread_row(bq_v, bq_ref)
    spread_row(bkv_v, bkv_ref)

    for s in range(steps):
        x_copies[s].wait()

        @pl.loop(0, group // PACK)
        def _(r):
            at = pl.ds(pl.multiple_of(r * PACK, PACK), PACK)
            x = x_v[s, at, :].astype(F32)
            mean = jnp.mean(x, axis=-1, keepdims=True)
            centered = x - mean
            var = jnp.mean(centered * centered, axis=-1, keepdims=True)
            scaled = centered * lax.rsqrt(var + LN_EPS)
            h = (scaled * gain_v[...] + bias_v[...]).astype(BF16)
            h_v[pl.ds(pl.multiple_of(s * group + r * PACK, PACK), PACK), :] = h

    depth = width // 8

    def product(total_ref, w_v):
        total_ref[...] = jnp.zeros_like(total_ref)

        @pl.loop(0, width // depth)
        def _(c):
            at = pl.ds(pl.multiple_of(c * depth, depth), depth)
            total_ref[...] += mm(h_v[:, at], w_v[at, :])

    wkv_copy.wait()
    product(kv_acc, wkv_v)
    kv = (kv_acc[...] + bkv_v[...]).astype(BF16)
    pad = fresh.shape[0] // local
    row = iota((local * pad, 1), 0)
    fresh[...] = mm(one_hot(local * pad, total, (row % pad) * group + me * local + row // pad, row % pad < steps), kv)
    window = 2 * PACK
    for c in (0, 1):
        for i in range(local):
            mid = caches[c][1]
            seq_len = lens_ref[i]
            start = jnp.minimum((seq_len // PACK) * PACK, cache_len - window)
            at = pl.ds(pl.multiple_of(start, PACK), window)
            pos = iota((window, head_dim), 0) + start
            ins[c][i].wait()
            value = mid[i, at, :].astype(F32)
            for s in range(steps):
                new = fresh[i * pad + s:i * pad + s + 1, c * head_dim:(c + 1) * head_dim]
                value = jnp.where(pos == seq_len + s, new, value)
            mid[i, at, :] = value.astype(BF16)
            outs[c][i].start()

    wq_copy.wait()
    product(acc, wq_v)
    q = (acc[...] + bq_v[...]).astype(BF16)
    share = local // PARTS
    for part in range(PARTS):
        pack_rows(
            q, lambda dest, r: (r % steps) * group + dest * local + part * share + r // steps,
            n, share * steps, pieces_ref.at[part])
    for c in (0, 1):
        for copy in outs[c]:
            copy.wait()


def group_kernel(n, steps, block, lens_ref, pieces_hbm, k_hbm, v_hbm, x_hbm, wo_hbm, bo_ref, y_hbm,
                 pieces_v, q_recv, q_v, k_v, v_v, scores, heads_v, o_send, o_recv, a_v, wo_v, x_v, rest_v, bo_v,
                 part_v, pair_send, pair_recv, rs_send, rs_recv, y_v,
                 in_sem, k_sem, v_sem, wo_sem, q_ssem, q_rsem, o_ssem, o_rsem, pair_ssem, pair_rsem,
                 rs_ssem, rs_rsem, ag_ssem, ag_rsem, d2d_ssem, d2d_rsem, out_sem):
    me = lax.axis_index('tp')
    local, cache_len, head_dim = k_v.shape
    share = local // PARTS
    rows = share * steps
    per_seq = n * steps
    total = share * per_seq
    depth = a_v.shape[2]
    heads = depth // head_dim
    cols = wo_v.shape[2]
    chips = n // 2
    far = chips // 2
    chip = me // 2
    core = me % 2
    mate = me + 1 - 2 * core
    group = local * n

    barrier = pltpu.get_barrier_semaphore()
    for k in range(1, n):
        pl.semaphore_signal(barrier, inc=1, device_id=peer(lax.rem(me + k, n)), device_id_type=MESH)

    def block_at(index):
        return pl.ds(pl.multiple_of(index * cols, LANES), cols)

    pieces_copy = pltpu.make_async_copy(pieces_hbm, pieces_v, in_sem.at[0])
    pieces_copy.start()
    x_copy = pltpu.make_async_copy(x_hbm.at[:, block_at(me)], x_v, in_sem.at[1])
    x_copy.start()

    cache_in = [(pltpu.make_async_copy(k_hbm.at[i], k_v.at[i], k_sem.at[i]),
                 pltpu.make_async_copy(v_hbm.at[i], v_v.at[i], v_sem.at[i])) for i in range(local)]
    for k_copy, v_copy in cache_in:
        k_copy.start()
        v_copy.start()
    offsets = [far]
    for k in range(far - 1, 0, -1):
        offsets += [k, chips - k]
    offsets.append(0)
    wo_copies = []
    for pos, off in enumerate(offsets):
        dest = lax.rem(chip + off, chips)
        for side, dev in enumerate((2 * dest + 1 - core, 2 * dest + core)):
            copy = pltpu.make_async_copy(wo_hbm.at[:, block_at(dev)], wo_v.at[2 * pos + side], wo_sem.at[2 * pos + side])
            copy.start()
            wo_copies.append(copy)

    bo_v[...] = bo_ref[...].astype(F32)
    tiles = cols // LANES
    bias = jnp.concatenate([bo_v[pl.ds(me * tiles + j, 1), :] for j in range(tiles)], axis=1)
    x_copy.wait()
    row = iota((total, 1), 0)
    for part in range(PARTS):
        source = (row // (n * share)) * group + ((row // share) % n) * local + part * share + row % share
        rest_v[part] = mm(one_hot(total, steps * group, source), x_v[...]) + bias

    def exchange(part, send_buf, recv_buf, send_sem, recv_sem):
        mine = pl.ds(pl.multiple_of(me * PACK, PACK), PACK)
        copies = []
        for k in sorted(range(1, n), key=lambda k: -min(k, n - k)):
            dest = lax.rem(me + k, n)
            copy = pltpu.make_async_remote_copy(
                src_ref=send_buf.at[part, pl.ds(pl.multiple_of(dest * PACK, PACK), PACK)],
                dst_ref=recv_buf.at[part, mine],
                send_sem=send_sem.at[part, k], recv_sem=recv_sem.at[part, k],
                device_id=peer(dest), device_id_type=MESH)
            copy.start()
            copies.append(copy)
        recv_buf[part, mine] = send_buf[part, mine]
        return copies

    pieces_copy.wait()
    pl.semaphore_wait(barrier, n - 1)
    q_copies = [exchange(part, pieces_v, q_recv, q_ssem, q_rsem) for part in range(PARTS)]

    n_rows = heads * per_seq
    factor = head_dim ** -0.5 * 1.4426950408889634
    col_step = iota((n_rows, block), 1) - iota((n_rows, block), 0) % steps

    def fold(value, op):
        out = value[:, :LANES]
        for c in range(1, block // LANES):
            out = op(out, value[:, c * LANES:(c + 1) * LANES])
        return out

    def attend(part):
        for copy in q_copies[part]:
            copy.wait_recv()
        by_head = unpack_rows(
            q_recv.at[part], total, heads,
            lambda row: ((row % per_seq) // steps, (row // per_seq) * steps + row % steps), rows)
        for i in range(share):
            for head in range(heads):
                q_v[i, head * per_seq:(head + 1) * per_seq, :] = by_head[head][i * per_seq:(i + 1) * per_seq]

        for copy in cache_in[part * share:(part + 1) * share]:
            copy[0].wait()
            copy[1].wait()

        @pl.loop(0, share)
        def _(i):
            seq = part * share + i
            seq_len = lens_ref[seq]
            q = q_v[i]
            top = jnp.full((n_rows, LANES), -jnp.inf, F32)
            for j in range(cache_len // block):
                at = slice(j * block, (j + 1) * block)
                t = lax.dot_general(q, k_v[seq, at, :], (((1,), (1,)), ((), ())), preferred_element_type=F32)
                t = jnp.where(col_step <= seq_len - j * block, t, -jnp.inf)
                scores[:, at] = t
                top = jnp.maximum(top, fold(t, jnp.maximum))
            top = jnp.max(top, axis=-1, keepdims=True)
            den = jnp.zeros((n_rows, LANES), F32)
            num = jnp.zeros((n_rows, head_dim), F32)
            for j in range(cache_len // block):
                at = slice(j * block, (j + 1) * block)
                p = jnp.exp2((scores[:, at] - top) * factor)
                num = num + mm(p.astype(BF16), v_v[seq, at, :])
                den = den + fold(p, jnp.add)
            out = (num / jnp.sum(den, axis=-1, keepdims=True)).astype(BF16)
            to = pl.ds(pl.multiple_of(i * per_seq, PACK), per_seq)
            for head in range(heads):
                heads_v[to, head * LANES:(head + 1) * LANES] = out[head * per_seq:(head + 1) * per_seq]

        pack_rows(
            heads_v[...], lambda dest, r: (r // steps) * per_seq + dest * steps + r % steps, n, rows, o_send.at[part])
        return exchange(part, o_send, o_recv, o_ssem, o_rsem)

    o_copies = [attend(part) for part in range(PARTS)]

    cut = (total // 2 + PACK - 1) // PACK * PACK
    halves = (pl.ds(0, cut), pl.ds(cut, total - cut))
    sign = (-1, 1)
    nexts = [2 * lax.rem(chip + chips + sign[d], chips) + core for d in (0, 1)]
    own = 2 * chip + core
    pair_copies = {}
    arrived = set()
    rs_copies = {}
    ag_copies = {}
    d2d_copies = []
    out_copies = []
    todo = {part: list(offsets) for part in range(PARTS)}

    def collect(part):
        for copy in o_copies[part]:
            copy.wait_recv()
        by_head = unpack_rows(
            o_recv.at[part], total, heads,
            lambda row: ((row // share) % n, (row % share) * steps + row // (n * share)), rows)
        for head in range(heads):
            a_v[part, :, head * LANES:(head + 1) * LANES] = by_head[head]

    def multiply(part, off):
        todo[part].remove(off)
        pos = offsets.index(off)
        if part == 0:
            wo_copies[2 * pos].wait()
        pair_send[part, pos] = mm(a_v[part], wo_v[2 * pos]).astype(BF16)
        copy = pltpu.make_async_remote_copy(
            src_ref=pair_send.at[part, pos], dst_ref=pair_recv.at[part, pos], send_sem=pair_ssem.at[part, pos],
            recv_sem=pair_rsem.at[part, pos], device_id=peer(mate), device_id_type=MESH)
        copy.start()
        pair_copies[part, off] = copy
        if part == 0:
            wo_copies[2 * pos + 1].wait()
        part_v[part, pos] = mm(a_v[part], wo_v[2 * pos + 1])

    def chip_sum(part, off, u):
        pos = offsets.index(off)
        if (part, off) not in arrived:
            pair_copies[part, off].wait_recv()
            arrived.add((part, off))
        return part_v[part, pos, halves[u], :] + pair_recv[part, pos, halves[u], :].astype(F32)

    def hops(part, d):
        return far if part == d else far - 1

    def reduce_stage(part, stage):
        for u in (0, 1):
            for d in (0, 1):
                k = hops(part, d) - stage
                if k < 1:
                    continue
                value = chip_sum(part, (sign[d] * k) % chips, u)
                if stage:
                    rs_copies[part, d, stage - 1, u].wait_recv()
                    value = value + rs_recv[part, d, stage - 1, halves[u], :].astype(F32)
                rs_send[part, d, stage, halves[u], :] = value.astype(BF16)
                copy = pltpu.make_async_remote_copy(
                    src_ref=rs_send.at[part, d, stage, halves[u]], dst_ref=rs_recv.at[part, d, stage, halves[u]],
                    send_sem=rs_ssem.at[part, d, stage, u], recv_sem=rs_rsem.at[part, d, stage, u],
                    device_id=peer(nexts[d]), device_id_type=MESH)
                copy.start()
                rs_copies[part, d, stage, u] = copy

    def gather_send(part, d, stage, index, u):
        at = y_v.at[part, index, halves[u]]
        copy = pltpu.make_async_remote_copy(
            src_ref=at, dst_ref=at, send_sem=ag_ssem.at[part, d, stage, u], recv_sem=ag_rsem.at[part, d, stage, u],
            device_id=peer(nexts[d]), device_id_type=MESH)
        copy.start()
        ag_copies[part, d, stage, u] = copy

    def place_out(part, index, sem):
        out = pltpu.make_async_copy(
            y_v.at[part, index], y_hbm.at[pl.ds(part * total, total), block_at(index)], sem)
        out.start()
        out_copies.append(out)

    def spread(part, index, hop):
        at = y_v.at[part, index]
        copy = pltpu.make_async_remote_copy(
            src_ref=at, dst_ref=at, send_sem=d2d_ssem.at[part, hop], recv_sem=d2d_rsem.at[part, hop],
            device_id=peer(mate), device_id_type=MESH)
        copy.start()
        d2d_copies.append((copy, part, index + 1 - 2 * core, hop))
        place_out(part, index, out_sem.at[0, part, hop])

    def own_stage(part):
        for u in (0, 1):
            value = rest_v[part, halves[u], :] + chip_sum(part, 0, u)
            for d in (0, 1):
                stage = hops(part, d) - 1
                rs_copies[part, d, stage, u].wait_recv()
                value = value + rs_recv[part, d, stage, halves[u], :].astype(F32)
            y_v[part, own, halves[u], :] = value.astype(BF16)
            for d in (0, 1):
                gather_send(part, d, 0, own, u)
        spread(part, own, 0)

    def gather_stage(part, stage):
        for u in (0, 1):
            for d in (0, 1):
                if stage >= hops(part, d):
                    continue
                hop = (-sign[d] * (stage + 1)) % chips
                index = 2 * lax.rem(chip + hop, chips) + core
                ag_copies[part, d, stage, u].wait_recv()
                if stage + 1 < hops(part, d):
                    gather_send(part, d, stage + 1, index, u)
                if u == 1:
                    spread(part, index, hop)

    def stage_of(part, s):
        if s < far:
            reduce_stage(part, s)
        elif s == far:
            own_stage(part)
        elif s <= 2 * far:
            gather_stage(part, s - far - 1)

    for part in range(PARTS):
        collect(part)
        first = [far] + [(sign[1 - part] * (far - 1)) % chips]
        for off in first:
            multiply(part, off)
        for off in list(todo[part])[:2]:
            multiply(part, off)
        reduce_stage(part, 0)
        for off in list(todo[part]):
            multiply(part, off)
    for s in range(1, 2 * far + 2):
        for part in range(PARTS):
            if s > part:
                stage_of(part, s - part)
    for copy, part, other, hop in d2d_copies:
        copy.wait_recv()
        place_out(part, other, out_sem.at[1, part, hop])
    for copies in q_copies + o_copies:
        for copy in copies:
            copy.wait_send()
    for copy in list(pair_copies.values()) + list(rs_copies.values()) + list(ag_copies.values()):
        copy.wait_send()
    for copy, _, _, _ in d2d_copies:
        copy.wait_send()
    for out in out_copies:
        out.wait()


def order_kernel(n, local, y_ref, out_ref, hot_v):
    steps, group, cols = out_ref.shape
    total = steps * group
    share = local // PARTS

    @pl.when(pl.program_id(0) == 0)
    def _():
        row = iota((total, 1), 0)
        step, seq = row // group, row % group
        dev, i = seq // local, seq % local
        index = (i // share) * (total // PARTS) + step * (n * share) + dev * share + i % share
        hot_v[...] = one_hot(total, total, index)

    out_ref[...] = mm(hot_v[...], y_ref[...]).astype(BF16).reshape(steps, group, cols)


def solution(mesh):
    n = mesh.shape['tp']
    vmem = pl.BlockSpec(memory_space=pltpu.VMEM)
    smem = pl.BlockSpec(memory_space=pltpu.SMEM)
    anywhere = pl.BlockSpec(memory_space=pl.ANY)
    dma = pltpu.SemaphoreType.DMA

    def by_lanes(vector):
        return vector.reshape(-1, LANES)

    def local_block(x_steps, seq_lens, k_cache, v_cache, ln_gain, ln_bias, w_q, b_q, w_kv, b_kv, w_out, b_out):
        steps, group, width = x_steps.shape
        local, cache_len, head_dim = k_cache.shape
        total = steps * group
        q_cols = w_q.shape[1]
        kv_cols = w_kv.shape[1]
        heads = q_cols // head_dim
        per_seq = n * steps
        share = local // PARTS
        piece_cols = -(-share * steps * heads // PACK) * LANES
        piece_shape = (PARTS, n * PACK, piece_cols)
        pieces, k_out, v_out = pl.pallas_call(
            functools.partial(local_kernel, n),
            name='local',
            out_shape=(
                jax.ShapeDtypeStruct(piece_shape, BF16),
                jax.ShapeDtypeStruct(k_cache.shape, BF16),
                jax.ShapeDtypeStruct(v_cache.shape, BF16),
            ),
            in_specs=[smem, anywhere, vmem, vmem, anywhere, vmem, anywhere, vmem, anywhere, anywhere],
            out_specs=(vmem, anywhere, anywhere),
            scratch_shapes=[
                pltpu.VMEM((steps, group, width), BF16),
                pltpu.VMEM((total, width), BF16),
                pltpu.VMEM((width, q_cols), BF16),
                pltpu.VMEM((width, kv_cols), BF16),
                pltpu.VMEM(k_cache.shape, BF16),
                pltpu.VMEM(v_cache.shape, BF16),
                pltpu.VMEM((total, q_cols), F32),
                pltpu.VMEM((total, kv_cols), F32),
                pltpu.VMEM((1, width), F32),
                pltpu.VMEM((1, width), F32),
                pltpu.VMEM((1, q_cols), F32),
                pltpu.VMEM((1, kv_cols), F32),
                pltpu.VMEM((local * 8, kv_cols), F32),
                dma((steps,)), dma((2,)), dma((2, local)), dma((2, local)),
            ],
            compiler_params=pltpu.CompilerParams(vmem_limit_bytes=VMEM_LIMIT),
        )(seq_lens, x_steps, by_lanes(ln_gain), by_lanes(ln_bias), w_q, by_lanes(b_q), w_kv, by_lanes(b_kv), k_cache, v_cache)

        block = cache_len // 3 if cache_len % (3 * LANES) == 0 else cache_len
        cols = width // n
        chips = n // 2
        far = chips // 2
        rows = total // PARTS
        y = pl.pallas_call(
            functools.partial(group_kernel, n, steps, block),
            name='group',
            out_shape=jax.ShapeDtypeStruct((total, width), BF16),
            in_specs=[smem, anywhere, anywhere, anywhere, anywhere, anywhere, vmem],
            out_specs=anywhere,
            scratch_shapes=[
                pltpu.VMEM(piece_shape, BF16),
                pltpu.VMEM(piece_shape, BF16),
                pltpu.VMEM((share, heads * per_seq, head_dim), BF16),
                pltpu.VMEM(k_cache.shape, BF16),
                pltpu.VMEM(v_cache.shape, BF16),
                pltpu.VMEM((heads * per_seq, cache_len), F32),
                pltpu.VMEM((rows, q_cols), BF16),
                pltpu.VMEM(piece_shape, BF16),
                pltpu.VMEM(piece_shape, BF16),
                pltpu.VMEM((PARTS, rows, q_cols), BF16),
                pltpu.VMEM((n, q_cols, cols), BF16),
                pltpu.VMEM((total, cols), BF16),
                pltpu.VMEM((PARTS, rows, cols), F32),
                pltpu.VMEM((width // LANES, LANES), F32),
                pltpu.VMEM((PARTS, chips, rows, cols), F32),
                pltpu.VMEM((PARTS, chips, rows, cols), BF16),
                pltpu.VMEM((PARTS, chips, rows, cols), BF16),
                pltpu.VMEM((PARTS, 2, far, rows, cols), BF16),
                pltpu.VMEM((PARTS, 2, far, rows, cols), BF16),
                pltpu.VMEM((PARTS, n, rows, cols), BF16),
                dma((2,)), dma((local,)), dma((local,)), dma((n,)),
                dma((PARTS, n)), dma((PARTS, n)), dma((PARTS, n)), dma((PARTS, n)),
                dma((PARTS, chips)), dma((PARTS, chips)),
                dma((PARTS, 2, far, 2)), dma((PARTS, 2, far, 2)), dma((PARTS, 2, far, 2)), dma((PARTS, 2, far, 2)),
                dma((PARTS, chips)), dma((PARTS, chips)), dma((2, PARTS, chips)),
            ],
            compiler_params=pltpu.CompilerParams(
                collective_id=0, has_side_effects=True, vmem_limit_bytes=VMEM_LIMIT),
        )(seq_lens, pieces, k_out, v_out, x_steps.reshape(total, width), w_out, by_lanes(b_out))

        wide = 2 * cols
        y_steps = pl.pallas_call(
            functools.partial(order_kernel, n, local),
            name='order',
            grid=(width // wide,),
            out_shape=jax.ShapeDtypeStruct(x_steps.shape, BF16),
            in_specs=[pl.BlockSpec((total, wide), lambda c: (0, c))],
            out_specs=pl.BlockSpec((steps, group, wide), lambda c: (0, 0, c)),
            scratch_shapes=[pltpu.VMEM((total, total), BF16)],
        )(y)
        return y_steps, k_out, v_out

    row_spec = P(('dp', 'tp'), None, None)
    return jax.shard_map(
        local_block,
        mesh=mesh,
        in_specs=(P(None, 'dp', None), P(('dp', 'tp')), row_spec, row_spec, P(None), P(None), P(None, 'tp'), P('tp'), P(None, None), P(None), P('tp', None), P(None)),
        out_specs=(P(None, 'dp', None), row_spec, row_spec),
        check_vma=False,
    )
```

time: 264 us -> 107 us (0.41)
  waiting for transfers between devices: 109 us -> 0 us
  Pallas kernels: 0 us -> 106 us
  matrix products: 53.3 us -> 0 us
  starting transfers between devices: 43.2 us -> 0 us
  other arithmetic: 33.6 us -> 0 us
  between operations: 14.5 us -> 0.65 us
  local copies, waits for them, and re-layouts: 9.18 us -> 0 us
    pallas_call x0 -> x3, Pallas kernels: none -> 106 us  [the longest x1 79.9 us: local_block(): pl.pallas_call(functools.partial(group_kernel, n, steps, block), name='gr...]
    psum x1 -> x0, waiting for transfers between devices: 102 us -> none  [local_block(): proj_sum = lax.psum(proj_part, 'tp')]
    dot_general x20 -> x0, matrix products: 53.3 us -> none  [the longest x3 16 us: attend(): jnp.einsum('bhd,btd->bht', q_rows, k_rows, preferred_element_type=jnp.flo...]
    all_to_all x6 -> x0, starting transfers between devices: 42.9 us -> none  [the longest x3 21.8 us: local_block(): q_local = lax.all_to_all(q_part, 'tp', 0, 1, tiled=True)]
    select_n x1 -> x0, other arithmetic: 11.7 us -> none  [write_cache(): jnp.where((offsets == slot_idx)[:, :, None], fresh_rows[:, slot_idx:slot_...]
    reduce_sum x7 -> x0, other arithmetic: 9.95 us -> none  [the longest x3 6.02 us: attend(): jnp.sum(old_weights, axis=-1, keepdims=True)]
    another operation x7 -> x0, other arithmetic: 7.51 us -> none  [the longest x2 6.3 us: local_block(): jnp.stack(outputs)]
    all_to_all x6 -> x0, waiting for transfers between devices: 7.2 us -> none  [the longest x3 6.61 us: local_block(): q_local = lax.all_to_all(q_part, 'tp', 0, 1, tiled=True)]
  transfers between devices with their start and end apart: 7 -> 0, of which waited for: 3 -> 0; matrix products, arithmetic and copies ran while one was open for 24% -> 0% of each run, Pallas kernels for 0% -> 0%
where the time goes in v2:
time: 107 us
  Pallas kernels  106 us (99%)
    pallas_call x1, Pallas kernels, local_block(): pl.pallas_call(functools.partial(group_kernel, n, steps, block), name='gr...  79.9 us
    pallas_call x1, Pallas kernels, local_block(): pl.pallas_call(functools.partial(local_kernel, n), name='local', out_shap...  18.2 us
    pallas_call x1, Pallas kernels, local_block(): pl.pallas_call(functools.partial(order_kernel, n, local), name='order', g...  7.93 us

profile of v2, /device:TPU:21, one launch (start us, length us, event | category | flops | bytes accessed | tf_op | source)
XLA Modules:
  0.0 106.6 jit_solution(6759817665568609839)
XLA Ops:
  0.6 18.2 %local.1 = (bf16[2,256,256]{2,1,0:T(8,128)(2,1)}, bf16[6,3072,128]{2,1,0:T(8,128)(2,1)}, bf16[6,3072,128]{2,1,0:T(8,128)(2,1)}) custom-call(s32[6]{0:T(128)} %lens_ref.3, bf16[3,96,6144]{2,1,0:T(8,128)(2,1)} %x_hbm.1, bf16[48,128]{1,0:T(8,128)(2,1)} %bitcast.7, bf16[48,128]{1,0:T(8,128)(2,1)} %bitcast.8, bf16[6144,384]{1,0:T(8,128)(2,1)} %wq_hbm.1, ...), custom_call_target="tpu_custom_call" | custom-call | tf_op jit(solution)/shard_map/local/pallas_call | solution.py:477
  18.8 79.9 %group.1.y_ref = bf16[288,6144]{1,0:T(8,128)(2,1)} custom-call(s32[6]{0:T(128)} %lens_ref.3, bf16[2,256,256]{2,1,0:T(8,128)(2,1)} %get-tuple-element.6.pieces_hbm, bf16[6,3072,128]{2,1,0:T(8,128)(2,1)} %get-tuple-element.4.k_hbm, bf16[6,3072,128]{2,1,0:T(8,128)(2,1)} %get-tuple-element.5.v_hbm, bf16[288,6144]{1,0:T(8,128)(2,1)} %bitcast.6, ...), custom_call_target="tpu_custom_call" | custom-call | tf_op jit(solution)/shard_map/group/pallas_call | solution.py:511
  98.7 7.9 %order.1 = bf16[3,96,6144]{2,1,0:T(8,128)(2,1)} custom-call(bf16[288,6144]{1,0:T(8,128)(2,1)} %group.1.y_ref), custom_call_target="tpu_custom_call" | custom-call | tf_op jit(solution)/shard_map/order/pallas_call | solution.py:549

commit v3 on v2

--- a/solution.py
+++ b/solution.py
@@ -12,6 +12,8 @@
 PACK = 16
 PARTS = 2
 VMEM_LIMIT = 60 * 1024 * 1024
+GROUP_LIMIT = 44 * 1024 * 1024
+ORDER_LIMIT = 16 * 1024 * 1024
 MESH = pl.DeviceIdType.MESH
 F32 = jnp.float32
 BF16 = jnp.bfloat16
@@ -38,33 +40,38 @@
     return range(head * rows // PACK, ((head + 1) * rows - 1) // PACK + 1)
 
 
-def pack_rows(src, source_row, n, rows, send_buf):
-    total, width = src.shape
-    heads = width // LANES
+def pairs_of(heads, rows):
+    return [(tile, head) for head in range(heads) for tile in tiles_of(head, rows)]
+
+
+def pack_hots(total, heads, source_row, n, rows):
     p = iota((n * PACK, 1), 0)
     dest, slot = p // PACK, p % PACK
-    for tile in range(send_buf.shape[-1] // LANES):
+    for tile, head in pairs_of(heads, rows):
         unit = tile * PACK + slot
-        index = source_row(dest, unit % rows)
-        value = jnp.zeros((n * PACK, LANES), F32)
-        for head in range(heads):
-            if tile in tiles_of(head, rows):
-                hot = one_hot(n * PACK, total, index, unit // rows == head)
-                value += mm(hot, src[:, head * LANES:(head + 1) * LANES])
-        send_buf[:, tile * LANES:(tile + 1) * LANES] = value.astype(BF16)
-
-
-def unpack_rows(recv_buf, total, heads, place, rows):
+        yield one_hot(n * PACK, total, source_row(dest, unit % rows), unit // rows == head)
+
+
+def pack_rows(src, hots, heads, rows, send_buf):
+    value = {}
+    for (tile, head), hot in zip(pairs_of(heads, rows), hots):
+        value[tile] = value.get(tile, 0.0) + mm(hot, src[:, head * LANES:(head + 1) * LANES])
+    for tile in value:
+        send_buf[:, tile * LANES:(tile + 1) * LANES] = value[tile].astype(BF16)
+
+
+def unpack_hots(n, total, heads, place, rows):
     source, row = place(iota((total, 1), 0))
-    out = []
-    for head in range(heads):
+    for tile, head in pairs_of(heads, rows):
         unit = head * rows + row
-        value = jnp.zeros((total, LANES), F32)
-        for tile in tiles_of(head, rows):
-            hot = one_hot(total, recv_buf.shape[0], source * PACK + unit % PACK, unit // PACK == tile)
-            value += mm(hot, recv_buf[:, tile * LANES:(tile + 1) * LANES])
-        out.append(value.astype(BF16))
-    return out
+        yield one_hot(total, n * PACK, source * PACK + unit % PACK, unit // PACK == tile)
+
+
+def unpack_rows(recv_buf, hots, heads, rows):
+    value = {}
+    for (tile, head), hot in zip(pairs_of(heads, rows), hots):
+        value[head] = value.get(head, 0.0) + mm(hot, recv_buf[:, tile * LANES:(tile + 1) * LANES])
+    return [value[head].astype(BF16) for head in range(heads)]
 
 
 def spread_row(row_ref, src_ref):
@@ -89,8 +96,10 @@
            for c, (src, mid, _) in enumerate(caches)]
     outs = [[pltpu.make_async_copy(mid.at[i], dst.at[i], out_sem.at[c, i]) for i in range(local)]
             for c, (_, mid, dst) in enumerate(caches)]
-    for copy in x_copies + [wkv_copy] + ins[0] + ins[1] + [wq_copy]:
+    for copy in x_copies + [wkv_copy, wq_copy]:
         copy.start()
+    for copy in ins[0] + ins[1]:
+        copy.start(priority=1)
     spread_row(gain_v, gain_ref)
     spread_row(bias_v, bias_ref)
     spread_row(bq_v, bq_ref)
@@ -140,16 +149,17 @@
                 new = fresh[i * pad + s:i * pad + s + 1, c * head_dim:(c + 1) * head_dim]
                 value = jnp.where(pos == seq_len + s, new, value)
             mid[i, at, :] = value.astype(BF16)
-            outs[c][i].start()
+            outs[c][i].start(priority=1)
 
     wq_copy.wait()
     product(acc, wq_v)
     q = (acc[...] + bq_v[...]).astype(BF16)
     share = local // PARTS
     for part in range(PARTS):
-        pack_rows(
-            q, lambda dest, r: (r % steps) * group + dest * local + part * share + r // steps,
-            n, share * steps, pieces_ref.at[part])
+        hots = pack_hots(
+            total, q_cols // LANES,
+            lambda dest, r: (r % steps) * group + dest * local + part * share + r // steps, n, share * steps)
+        pack_rows(q, hots, q_cols // LANES, share * steps, pieces_ref.at[part])
     for c in (0, 1):
         for copy in outs[c]:
             copy.wait()
@@ -157,7 +167,7 @@
 
 def group_kernel(n, steps, block, lens_ref, pieces_hbm, k_hbm, v_hbm, x_hbm, wo_hbm, bo_ref, y_hbm,
                  pieces_v, q_recv, q_v, k_v, v_v, scores, heads_v, o_send, o_recv, a_v, wo_v, x_v, rest_v, bo_v,
-                 part_v, pair_send, pair_recv, rs_send, rs_recv, y_v,
+                 part_v, pair_send, pair_recv, rs_send, rs_recv, y_v, pack_v, q_hot, o_hot,
                  in_sem, k_sem, v_sem, wo_sem, q_ssem, q_rsem, o_ssem, o_rsem, pair_ssem, pair_rsem,
                  rs_ssem, rs_rsem, ag_ssem, ag_rsem, d2d_ssem, d2d_rsem, out_sem):
     me = lax.axis_index('tp')
@@ -214,6 +224,20 @@
         source = (row // (n * share)) * group + ((row // share) % n) * local + part * share + row % share
         rest_v[part] = mm(one_hot(total, steps * group, source), x_v[...]) + bias
 
+    def fill(ref, hots):
+        for j, hot in enumerate(hots):
+            ref[j] = hot
+
+    def held(ref):
+        return [ref[j] for j in range(ref.shape[0])]
+
+    fill(q_hot, unpack_hots(
+        n, total, heads, lambda row: ((row % per_seq) // steps, (row // per_seq) * steps + row % steps), rows))
+    fill(pack_v, pack_hots(
+        total, heads, lambda dest, r: (r // steps) * per_seq + dest * steps + r % steps, n, rows))
+    fill(o_hot, unpack_hots(
+        n, total, heads, lambda row: ((row // share) % n, (row % share) * steps + row // (n * share)), rows))
+
     def exchange(part, send_buf, recv_buf, send_sem, recv_sem):
         mine = pl.ds(pl.multiple_of(me * PACK, PACK), PACK)
         copies = []
@@ -246,9 +270,7 @@
     def attend(part):
         for copy in q_copies[part]:
             copy.wait_recv()
-        by_head = unpack_rows(
-            q_recv.at[part], total, heads,
-            lambda row: ((row % per_seq) // steps, (row // per_seq) * steps + row % steps), rows)
+        by_head = unpack_rows(q_recv.at[part], held(q_hot), heads, rows)
         for i in range(share):
             for head in range(heads):
                 q_v[i, head * per_seq:(head + 1) * per_seq, :] = by_head[head][i * per_seq:(i + 1) * per_seq]
@@ -282,8 +304,7 @@
             for head in range(heads):
                 heads_v[to, head * LANES:(head + 1) * LANES] = out[head * per_seq:(head + 1) * per_seq]
 
-        pack_rows(
-            heads_v[...], lambda dest, r: (r // steps) * per_seq + dest * steps + r % steps, n, rows, o_send.at[part])
+        pack_rows(heads_v[...], held(pack_v), heads, rows, o_send.at[part])
         return exchange(part, o_send, o_recv, o_ssem, o_rsem)
 
     o_copies = [attend(part) for part in range(PARTS)]
@@ -295,6 +316,7 @@
     own = 2 * chip + core
     pair_copies = {}
     arrived = set()
+    loaded = set()
     rs_copies = {}
     ag_copies = {}
     d2d_copies = []
@@ -304,16 +326,16 @@
     def collect(part):
         for copy in o_copies[part]:
             copy.wait_recv()
-        by_head = unpack_rows(
-            o_recv.at[part], total, heads,
-            lambda row: ((row // share) % n, (row % share) * steps + row // (n * share)), rows)
+        by_head = unpack_rows(o_recv.at[part], held(o_hot), heads, rows)
         for head in range(heads):
             a_v[part, :, head * LANES:(head + 1) * LANES] = by_head[head]
 
     def multiply(part, off):
         todo[part].remove(off)
         pos = offsets.index(off)
-        if part == 0:
+        first = off not in loaded
+        loaded.add(off)
+        if first:
             wo_copies[2 * pos].wait()
         pair_send[part, pos] = mm(a_v[part], wo_v[2 * pos]).astype(BF16)
         copy = pltpu.make_async_remote_copy(
@@ -321,7 +343,7 @@
             recv_sem=pair_rsem.at[part, pos], device_id=peer(mate), device_id_type=MESH)
         copy.start()
         pair_copies[part, off] = copy
-        if part == 0:
+        if first:
             wo_copies[2 * pos + 1].wait()
         part_v[part, pos] = mm(a_v[part], wo_v[2 * pos + 1])
 
@@ -409,20 +431,22 @@
         elif s <= 2 * far:
             gather_stage(part, s - far - 1)
 
+    def prepare(part, stage):
+        need = [(sign[d] * (hops(part, d) - stage)) % chips for d in (0, 1)] if stage < far - 1 else todo[part]
+        for off in list(need):
+            if off in todo[part]:
+                multiply(part, off)
+
     for part in range(PARTS):
         collect(part)
-        first = [far] + [(sign[1 - part] * (far - 1)) % chips]
-        for off in first:
-            multiply(part, off)
-        for off in list(todo[part])[:2]:
-            multiply(part, off)
-        reduce_stage(part, 0)
-        for off in list(todo[part]):
-            multiply(part, off)
+        prepare(part, 0)
+        prepare(part, 1)
+        stage_of(part, 0)
     for s in range(1, 2 * far + 2):
         for part in range(PARTS):
             if s > part:
                 stage_of(part, s - part)
+                prepare(part, s - part + 1)
     for copy, part, other, hop in d2d_copies:
         copy.wait_recv()
         place_out(part, other, out_sem.at[1, part, hop])
@@ -437,20 +461,20 @@
         out.wait()
 
 
-def order_kernel(n, local, y_ref, out_ref, hot_v):
-    steps, group, cols = out_ref.shape
-    total = steps * group
+def order_kernel(n, y_ref, out_ref, hot_v):
+    steps, group, _ = out_ref.shape
+    local = group // n
     share = local // PARTS
 
     @pl.when(pl.program_id(0) == 0)
     def _():
-        row = iota((total, 1), 0)
-        step, seq = row // group, row % group
+        seq = iota((group, 1), 0)
         dev, i = seq // local, seq % local
-        index = (i // share) * (total // PARTS) + step * (n * share) + dev * share + i % share
-        hot_v[...] = one_hot(total, total, index)
-
-    out_ref[...] = mm(hot_v[...], y_ref[...]).astype(BF16).reshape(steps, group, cols)
+        hot_v[...] = one_hot(group, group, (i // share) * (n * share) + dev * share + i % share)
+
+    for s in range(steps):
+        src = jnp.concatenate([y_ref[part, s] for part in range(PARTS)], axis=0)
+        out_ref[s] = mm(hot_v[...], src).astype(BF16)
 
 
 def solution(mesh):
@@ -459,6 +483,9 @@
     smem = pl.BlockSpec(memory_space=pltpu.SMEM)
     anywhere = pl.BlockSpec(memory_space=pl.ANY)
     dma = pltpu.SemaphoreType.DMA
+
+    def in_hbm(array):
+        return pltpu.with_memory_space_constraint(array, pltpu.HBM)
 
     def by_lanes(vector):
         return vector.reshape(-1, LANES)
@@ -508,6 +535,7 @@
         chips = n // 2
         far = chips // 2
         rows = total // PARTS
+        n_pairs = len(pairs_of(heads, share * steps))
         y = pl.pallas_call(
             functools.partial(group_kernel, n, steps, block),
             name='group',
@@ -535,6 +563,9 @@
                 pltpu.VMEM((PARTS, 2, far, rows, cols), BF16),
                 pltpu.VMEM((PARTS, 2, far, rows, cols), BF16),
                 pltpu.VMEM((PARTS, n, rows, cols), BF16),
+                pltpu.VMEM((n_pairs, n * PACK, rows), BF16),
+                pltpu.VMEM((n_pairs, rows, n * PACK), BF16),
+                pltpu.VMEM((n_pairs, rows, n * PACK), BF16),
                 dma((2,)), dma((local,)), dma((local,)), dma((n,)),
                 dma((PARTS, n)), dma((PARTS, n)), dma((PARTS, n)), dma((PARTS, n)),
                 dma((PARTS, chips)), dma((PARTS, chips)),
@@ -542,19 +573,21 @@
                 dma((PARTS, chips)), dma((PARTS, chips)), dma((2, PARTS, chips)),
             ],
             compiler_params=pltpu.CompilerParams(
-                collective_id=0, has_side_effects=True, vmem_limit_bytes=VMEM_LIMIT),
-        )(seq_lens, pieces, k_out, v_out, x_steps.reshape(total, width), w_out, by_lanes(b_out))
+                collective_id=0, has_side_effects=True, vmem_limit_bytes=GROUP_LIMIT),
+        )(seq_lens, in_hbm(pieces), in_hbm(k_out), in_hbm(v_out), in_hbm(x_steps.reshape(total, width)), in_hbm(w_out),
+          by_lanes(b_out))
 
         wide = 2 * cols
         y_steps = pl.pallas_call(
-            functools.partial(order_kernel, n, local),
+            functools.partial(order_kernel, n),
             name='order',
             grid=(width // wide,),
             out_shape=jax.ShapeDtypeStruct(x_steps.shape, BF16),
-            in_specs=[pl.BlockSpec((total, wide), lambda c: (0, c))],
+            in_specs=[pl.BlockSpec((PARTS, steps, group // PARTS, wide), lambda c: (0, 0, 0, c))],
             out_specs=pl.BlockSpec((steps, group, wide), lambda c: (0, 0, c)),
-            scratch_shapes=[pltpu.VMEM((total, total), BF16)],
-        )(y)
+            scratch_shapes=[pltpu.VMEM((group, group), BF16)],
+            compiler_params=pltpu.CompilerParams(vmem_limit_bytes=ORDER_LIMIT),
+        )(y.reshape(PARTS, steps, group // PARTS, width))
         return y_steps, k_out, v_out
 
     row_spec = P(('dp', 'tp'), None, None)

time: 107 us -> 102 us (0.953); the launches traced: 107 us -> 101 us
  Pallas kernels: 106 us -> 99.8 us
    pallas_call x1, Pallas kernels: 7.93 us -> 4.63 us  [local_block(): pl.pallas_call(functools.partial(order_kernel, n), name='order', grid=(wi...]
    pallas_call x1, Pallas kernels: 18.2 us -> 16.1 us  [local_block(): pl.pallas_call(functools.partial(local_kernel, n), name='local', out_shap...]
where the time goes in v3:
time: 102 us; the launch traced here: 101 us
  Pallas kernels  99.8 us (98%)
    pallas_call x1, Pallas kernels, local_block(): pl.pallas_call(functools.partial(group_kernel, n, steps, block), name='gr...  79.1 us
    pallas_call x1, Pallas kernels, local_block(): pl.pallas_call(functools.partial(local_kernel, n), name='local', out_shap...  16.1 us
    pallas_call x1, Pallas kernels, local_block(): pl.pallas_call(functools.partial(order_kernel, n), name='order', grid=(wi...  4.63 us

profile of v3, /device:TPU:21, one launch (start us, length us, event | category | flops | bytes accessed | tf_op | source)
XLA Modules:
  0.0 100.5 jit_solution(11127426306507895361)
XLA Ops:
  0.6 0.0 copy-start
  0.6 0.0 copy-start.1
  0.7 16.1 %local.1 = (bf16[2,256,256]{2,1,0:T(8,128)(2,1)}, bf16[6,3072,128]{2,1,0:T(8,128)(2,1)}, bf16[6,3072,128]{2,1,0:T(8,128)(2,1)}) custom-call(s32[6]{0:T(128)} %lens_ref.3, bf16[3,96,6144]{2,1,0:T(8,128)(2,1)} %x_hbm.1, bf16[48,128]{1,0:T(8,128)(2,1)} %bitcast.10, bf16[48,128]{1,0:T(8,128)(2,1)} %bitcast.11, bf16[6144,384]{1,0:T(8,128)(2,1)} %wq_hbm.1, ...), custom_call_target="tpu_custom_call" | custom-call | tf_op jit(solution)/shard_map/local/pallas_call | solution.py:504
  16.8 0.0 copy-done
  16.8 0.0 copy-done.1
  16.8 79.1 %group.1 = bf16[288,6144]{1,0:T(8,128)(2,1)S(1)} custom-call(s32[6]{0:T(128)S(1)} %copy-done.1, bf16[2,256,256]{2,1,0:T(8,128)(2,1)} %get-tuple-element.6.pieces_hbm, bf16[6,3072,128]{2,1,0:T(8,128)(2,1)} %get-tuple-element.4.k_hbm, bf16[6,3072,128]{2,1,0:T(8,128)(2,1)} %get-tuple-element.5.v_hbm, bf16[288,6144]{1,0:T(8,128)(2,1)} %bitcast.9, ...), custom_call_target="tpu_custom_call" | custom-call | tf_op jit(solution)/shard_map/group/pallas_call | solution.py:539
  95.9 4.6 %order.1 = bf16[3,96,6144]{2,1,0:T(8,128)(2,1)} custom-call(bf16[2,3,48,6144]{3,2,1,0:T(8,128)(2,1)S(1)} %bitcast.7), custom_call_target="tpu_custom_call" | custom-call | tf_op jit(solution)/shard_map/order/pallas_call | solution.py:581
Async XLA Ops:
  0.6 16.2 %copy-start = (bf16[6144]{0:T(1024)(128)(2,1)S(1)}, bf16[6144]{0:T(1024)(128)(2,1)}, u32[]{:S(2)}) copy-start(bf16[6144]{0:T(1024)(128)(2,1)} %param.23) | copy-start | bytes 36868
  0.6 16.2 %copy-start.1 = (s32[6]{0:T(128)S(1)}, s32[6]{0:T(128)}, u32[]{:S(2)}) copy-start(s32[6]{0:T(128)} %lens_ref.3) | copy-start | bytes 76

commit v4 on v3

--- a/solution.py
+++ b/solution.py
@@ -72,6 +72,10 @@
     for (tile, head), hot in zip(pairs_of(heads, rows), hots):
         value[head] = value.get(head, 0.0) + mm(hot, recv_buf[:, tile * LANES:(tile + 1) * LANES])
     return [value[head].astype(BF16) for head in range(heads)]
+
+
+def cut_of(rows):
+    return -(-rows // (2 * PACK)) * PACK
 
 
 def spread_row(row_ref, src_ref):
@@ -309,7 +313,8 @@
 
     o_copies = [attend(part) for part in range(PARTS)]
 
-    cut = (total // 2 + PACK - 1) // PACK * PACK
+    cut = cut_of(total)
+    sizes = (cut, total - cut)
     halves = (pl.ds(0, cut), pl.ds(cut, total - cut))
     sign = (-1, 1)
     nexts = [2 * lax.rem(chip + chips + sign[d], chips) + core for d in (0, 1)]
@@ -354,34 +359,36 @@
             arrived.add((part, off))
         return part_v[part, pos, halves[u], :] + pair_recv[part, pos, halves[u], :].astype(F32)
 
-    def hops(part, d):
-        return far if part == d else far - 1
-
-    def reduce_stage(part, stage):
-        for u in (0, 1):
-            for d in (0, 1):
-                k = hops(part, d) - stage
-                if k < 1:
-                    continue
-                value = chip_sum(part, (sign[d] * k) % chips, u)
-                if stage:
-                    rs_copies[part, d, stage - 1, u].wait_recv()
-                    value = value + rs_recv[part, d, stage - 1, halves[u], :].astype(F32)
-                rs_send[part, d, stage, halves[u], :] = value.astype(BF16)
-                copy = pltpu.make_async_remote_copy(
-                    src_ref=rs_send.at[part, d, stage, halves[u]], dst_ref=rs_recv.at[part, d, stage, halves[u]],
-                    send_sem=rs_ssem.at[part, d, stage, u], recv_sem=rs_rsem.at[part, d, stage, u],
-                    device_id=peer(nexts[d]), device_id_type=MESH)
-                copy.start()
-                rs_copies[part, d, stage, u] = copy
-
-    def gather_send(part, d, stage, index, u):
+    def lone(part, d):
+        return d ^ part
+
+    plan = {
+        (part, d): [(far, lone(part, d))] + [(k, h) for k in range(far - 1, 0, -1) for h in (1 - lone(part, d), lone(part, d))]
+        for part in range(PARTS) for d in (0, 1)}
+    n_slots = 2 * far - 1
+
+    def reduce_slot(part, slot):
+        for d in (0, 1):
+            k, u = plan[part, d][slot]
+            value = chip_sum(part, (sign[d] * k) % chips, u)
+            if slot >= 2:
+                rs_copies[part, d, slot - 2].wait_recv()
+                value = value + rs_recv[part, d, slot - 2, :sizes[u], :].astype(F32)
+            rs_send[part, d, slot, :sizes[u], :] = value.astype(BF16)
+            copy = pltpu.make_async_remote_copy(
+                src_ref=rs_send.at[part, d, slot, pl.ds(0, sizes[u])], dst_ref=rs_recv.at[part, d, slot, pl.ds(0, sizes[u])],
+                send_sem=rs_ssem.at[part, d, slot], recv_sem=rs_rsem.at[part, d, slot],
+                device_id=peer(nexts[d]), device_id_type=MESH)
+            copy.start()
+            rs_copies[part, d, slot] = copy
+
+    def gather_send(part, d, slot, index, u):
         at = y_v.at[part, index, halves[u]]
         copy = pltpu.make_async_remote_copy(
-            src_ref=at, dst_ref=at, send_sem=ag_ssem.at[part, d, stage, u], recv_sem=ag_rsem.at[part, d, stage, u],
+            src_ref=at, dst_ref=at, send_sem=ag_ssem.at[part, d, slot], recv_sem=ag_rsem.at[part, d, slot],
             device_id=peer(nexts[d]), device_id_type=MESH)
         copy.start()
-        ag_copies[part, d, stage, u] = copy
+        ag_copies[part, d, slot] = copy
 
     def place_out(part, index, sem):
         out = pltpu.make_async_copy(
@@ -398,55 +405,59 @@
         d2d_copies.append((copy, part, index + 1 - 2 * core, hop))
         place_out(part, index, out_sem.at[0, part, hop])
 
-    def own_stage(part):
+    def own_step(part):
         for u in (0, 1):
             value = rest_v[part, halves[u], :] + chip_sum(part, 0, u)
             for d in (0, 1):
-                stage = hops(part, d) - 1
-                rs_copies[part, d, stage, u].wait_recv()
-                value = value + rs_recv[part, d, stage, halves[u], :].astype(F32)
+                slot = n_slots - 1 if lone(part, d) == u else n_slots - 2
+                rs_copies[part, d, slot].wait_recv()
+                value = value + rs_recv[part, d, slot, :sizes[u], :].astype(F32)
             y_v[part, own, halves[u], :] = value.astype(BF16)
+        for slot in (0, 1):
             for d in (0, 1):
-                gather_send(part, d, 0, own, u)
+                gather_send(part, d, slot, own, lone(part, d) if slot else 1 - lone(part, d))
         spread(part, own, 0)
 
-    def gather_stage(part, stage):
-        for u in (0, 1):
-            for d in (0, 1):
-                if stage >= hops(part, d):
-                    continue
-                hop = (-sign[d] * (stage + 1)) % chips
-                index = 2 * lax.rem(chip + hop, chips) + core
-                ag_copies[part, d, stage, u].wait_recv()
-                if stage + 1 < hops(part, d):
-                    gather_send(part, d, stage + 1, index, u)
-                if u == 1:
-                    spread(part, index, hop)
-
-    def stage_of(part, s):
-        if s < far:
-            reduce_stage(part, s)
-        elif s == far:
-            own_stage(part)
-        elif s <= 2 * far:
-            gather_stage(part, s - far - 1)
-
-    def prepare(part, stage):
-        need = [(sign[d] * (hops(part, d) - stage)) % chips for d in (0, 1)] if stage < far - 1 else todo[part]
+    landed = {}
+
+    def gather_slot(part, slot):
+        for d in (0, 1):
+            u = lone(part, d) if slot % 2 else 1 - lone(part, d)
+            hop = (-sign[d] * (slot // 2 + 1)) % chips
+            index = 2 * lax.rem(chip + hop, chips) + core
+            ag_copies[part, d, slot].wait_recv()
+            if slot + 2 < n_slots:
+                gather_send(part, d, slot + 2, index, u)
+            landed[part, hop] = landed.get((part, hop), 0) + 1
+            if landed[part, hop] == 2:
+                spread(part, index, hop)
+
+    def prepare(part, slot):
+        need = [(sign[d] * plan[part, d][slot][0]) % chips for d in (0, 1)] if slot < n_slots else todo[part]
         for off in list(need):
             if off in todo[part]:
                 multiply(part, off)
 
+    def step_of(part, s):
+        if 0 <= s < n_slots:
+            prepare(part, s + 2)
+            reduce_slot(part, s)
+        elif s == n_slots:
+            own_step(part)
+        elif n_slots < s <= 2 * n_slots:
+            gather_slot(part, s - n_slots - 1)
+
+    lag = 2
     for part in range(PARTS):
         collect(part)
         prepare(part, 0)
         prepare(part, 1)
-        stage_of(part, 0)
-    for s in range(1, 2 * far + 2):
+        if part == 0:
+            for s in range(lag):
+                step_of(0, s)
+    for s in range(lag, 2 * n_slots + 1 + lag):
         for part in range(PARTS):
-            if s > part:
-                stage_of(part, s - part)
-                prepare(part, s - part + 1)
+            step_of(part, s - part * lag)
     for copy, part, other, hop in d2d_copies:
         copy.wait_recv()
         place_out(part, other, out_sem.at[1, part, hop])
@@ -536,6 +547,7 @@
         far = chips // 2
         rows = total // PARTS
         n_pairs = len(pairs_of(heads, share * steps))
+        cut = cut_of(rows)
         y = pl.pallas_call(
             functools.partial(group_kernel, n, steps, block),
             name='group',
@@ -560,8 +572,8 @@
                 pltpu.VMEM((PARTS, chips, rows, cols), F32),
                 pltpu.VMEM((PARTS, chips, rows, cols), BF16),
                 pltpu.VMEM((PARTS, chips, rows, cols), BF16),
-                pltpu.VMEM((PARTS, 2, far, rows, cols), BF16),
-                pltpu.VMEM((PARTS, 2, far, rows, cols), BF16),
+                pltpu.VMEM((PARTS, 2, 2 * far - 1, cut, cols), BF16),
+                pltpu.VMEM((PARTS, 2, 2 * far - 1, cut, cols), BF16),
                 pltpu.VMEM((PARTS, n, rows, cols), BF16),
                 pltpu.VMEM((n_pairs, n * PACK, rows), BF16),
                 pltpu.VMEM((n_pairs, rows, n * PACK), BF16),
@@ -569,7 +581,8 @@
                 dma((2,)), dma((local,)), dma((local,)), dma((n,)),
                 dma((PARTS, n)), dma((PARTS, n)), dma((PARTS, n)), dma((PARTS, n)),
                 dma((PARTS, chips)), dma((PARTS, chips)),
-                dma((PARTS, 2, far, 2)), dma((PARTS, 2, far, 2)), dma((PARTS, 2, far, 2)), dma((PARTS, 2, far, 2)),
+                dma((PARTS, 2, 2 * far - 1)), dma((PARTS, 2, 2 * far - 1)),
+                dma((PARTS, 2, 2 * far - 1)), dma((PARTS, 2, 2 * far - 1)),
                 dma((PARTS, chips)), dma((PARTS, chips)), dma((2, PARTS, chips)),
             ],
             compiler_params=pltpu.CompilerParams(

time: 102 us -> 99.6 us (0.976)
  Pallas kernels: 99.8 us -> 97.3 us
    pallas_call x1, Pallas kernels: 79.1 us -> 76.5 us  [local_block(): pl.pallas_call(functools.partial(group_kernel, n, steps, block), name='gr...]
where the time goes in v4:
time: 99.6 us; the launch traced here: 98 us
  Pallas kernels  97.3 us (98%)
    pallas_call x1, Pallas kernels, local_block(): pl.pallas_call(functools.partial(group_kernel, n, steps, block), name='gr...  76.5 us
    pallas_call x1, Pallas kernels, local_block(): pl.pallas_call(functools.partial(local_kernel, n), name='local', out_shap...  16.1 us
    pallas_call x1, Pallas kernels, local_block(): pl.pallas_call(functools.partial(order_kernel, n), name='order', grid=(wi...  4.62 us

profile of v4, /device:TPU:21, one launch (start us, length us, event | category | flops | bytes accessed | tf_op | source)
XLA Modules:
  0.0 98.0 jit_solution(18378268625138484123)
XLA Ops:
  0.6 0.0 copy-start
  0.6 0.0 copy-start.1
  0.7 16.1 %local.1 = (bf16[2,256,256]{2,1,0:T(8,128)(2,1)}, bf16[6,3072,128]{2,1,0:T(8,128)(2,1)}, bf16[6,3072,128]{2,1,0:T(8,128)(2,1)}) custom-call(s32[6]{0:T(128)} %lens_ref.3, bf16[3,96,6144]{2,1,0:T(8,128)(2,1)} %x_hbm.1, bf16[48,128]{1,0:T(8,128)(2,1)} %bitcast.10, bf16[48,128]{1,0:T(8,128)(2,1)} %bitcast.11, bf16[6144,384]{1,0:T(8,128)(2,1)} %wq_hbm.1, ...), custom_call_target="tpu_custom_call" | custom-call | tf_op jit(solution)/shard_map/local/pallas_call | solution.py:515
  16.8 0.0 copy-done
  16.8 0.0 copy-done.1
  16.8 76.5 %group.1 = bf16[288,6144]{1,0:T(8,128)(2,1)S(1)} custom-call(s32[6]{0:T(128)S(1)} %copy-done.1, bf16[2,256,256]{2,1,0:T(8,128)(2,1)} %get-tuple-element.6.pieces_hbm, bf16[6,3072,128]{2,1,0:T(8,128)(2,1)} %get-tuple-element.4.k_hbm, bf16[6,3072,128]{2,1,0:T(8,128)(2,1)} %get-tuple-element.5.v_hbm, bf16[288,6144]{1,0:T(8,128)(2,1)} %bitcast.9, ...), custom_call_target="tpu_custom_call" | custom-call | tf_op jit(solution)/shard_map/group/pallas_call | solution.py:551
  93.3 4.6 %order.1 = bf16[3,96,6144]{2,1,0:T(8,128)(2,1)} custom-call(bf16[2,3,48,6144]{3,2,1,0:T(8,128)(2,1)S(1)} %bitcast.7), custom_call_target="tpu_custom_call" | custom-call | tf_op jit(solution)/shard_map/order/pallas_call | solution.py:594
Async XLA Ops:
  0.6 16.2 %copy-start = (bf16[6144]{0:T(1024)(128)(2,1)S(1)}, bf16[6144]{0:T(1024)(128)(2,1)}, u32[]{:S(2)}) copy-start(bf16[6144]{0:T(1024)(128)(2,1)} %param.23) | copy-start | bytes 36868
  0.6 16.2 %copy-start.1 = (s32[6]{0:T(128)S(1)}, s32[6]{0:T(128)}, u32[]{:S(2)}) copy-start(s32[6]{0:T(128)} %lens_ref.3) | copy-start | bytes 76

commit v5 on v4

--- a/solution.py
+++ b/solution.py
@@ -83,10 +83,11 @@
         row_ref[:, j * LANES:(j + 1) * LANES] = src_ref[j:j + 1, :].astype(F32)
 
 
-def local_kernel(n, lens_ref, x_hbm, gain_ref, bias_ref, wq_hbm, bq_ref, wkv_hbm, bkv_ref, k_hbm, v_hbm,
-                 pieces_ref, ko_hbm, vo_hbm,
+def local_kernel(n, lens_hbm, x_hbm, gain_hbm, bias_hbm, wq_hbm, bq_hbm, wkv_hbm, bkv_hbm, k_hbm, v_hbm,
+                 pieces_hbm, ko_hbm, vo_hbm,
                  x_v, h_v, wq_v, wkv_v, k_v, v_v, acc, kv_acc, gain_v, bias_v, bq_v, bkv_v, fresh,
-                 x_sem, w_sem, in_sem, out_sem):
+                 pieces_v, gain_ref, bias_ref, bq_ref, bkv_ref, lens_ref,
+                 x_sem, w_sem, in_sem, out_sem, small_sem, piece_sem):
     me = lax.axis_index('tp')
     steps, group, width = x_v.shape
     q_cols = wq_v.shape[1]
@@ -100,10 +101,14 @@
            for c, (src, mid, _) in enumerate(caches)]
     outs = [[pltpu.make_async_copy(mid.at[i], dst.at[i], out_sem.at[c, i]) for i in range(local)]
             for c, (_, mid, dst) in enumerate(caches)]
-    for copy in x_copies + [wkv_copy, wq_copy]:
+    small = [pltpu.make_async_copy(src, dst, small_sem.at[j]) for j, (src, dst) in enumerate((
+        (gain_hbm, gain_ref), (bias_hbm, bias_ref), (bq_hbm, bq_ref), (bkv_hbm, bkv_ref), (lens_hbm, lens_ref)))]
+    for copy in x_copies[:1] + small + x_copies[1:] + [wkv_copy, wq_copy]:
         copy.start()
     for copy in ins[0] + ins[1]:
         copy.start(priority=1)
+    for copy in small:
+        copy.wait()
     spread_row(gain_v, gain_ref)
     spread_row(bias_v, bias_ref)
     spread_row(bq_v, bq_ref)
@@ -159,19 +164,22 @@
     product(acc, wq_v)
     q = (acc[...] + bq_v[...]).astype(BF16)
     share = local // PARTS
+    pieces = []
     for part in range(PARTS):
         hots = pack_hots(
             total, q_cols // LANES,
             lambda dest, r: (r % steps) * group + dest * local + part * share + r // steps, n, share * steps)
-        pack_rows(q, hots, q_cols // LANES, share * steps, pieces_ref.at[part])
-    for c in (0, 1):
-        for copy in outs[c]:
-            copy.wait()
-
-
-def group_kernel(n, steps, block, lens_ref, pieces_hbm, k_hbm, v_hbm, x_hbm, wo_hbm, bo_ref, y_hbm,
+        pack_rows(q, hots, q_cols // LANES, share * steps, pieces_v.at[part])
+        piece = pltpu.make_async_copy(pieces_v.at[part], pieces_hbm.at[part], piece_sem.at[part])
+        piece.start()
+        pieces.append(piece)
+    for copy in outs[0] + outs[1] + pieces:
+        copy.wait()
+
+
+def group_kernel(n, steps, block, lens_hbm, pieces_hbm, k_hbm, v_hbm, x_hbm, wo_hbm, bo_hbm, y_hbm,
                  pieces_v, q_recv, q_v, k_v, v_v, scores, heads_v, o_send, o_recv, a_v, wo_v, x_v, rest_v, bo_v,
-                 part_v, pair_send, pair_recv, rs_send, rs_recv, y_v, pack_v, q_hot, o_hot,
+                 part_v, pair_send, pair_recv, rs_send, rs_recv, y_v, pack_v, q_hot, o_hot, bo_ref, lens_ref,
                  in_sem, k_sem, v_sem, wo_sem, q_ssem, q_rsem, o_ssem, o_rsem, pair_ssem, pair_rsem,
                  rs_ssem, rs_rsem, ag_ssem, ag_rsem, d2d_ssem, d2d_rsem, out_sem):
     me = lax.axis_index('tp')
@@ -201,6 +209,10 @@
     pieces_copy.start()
     x_copy = pltpu.make_async_copy(x_hbm.at[:, block_at(me)], x_v, in_sem.at[1])
     x_copy.start()
+    bo_copy = pltpu.make_async_copy(bo_hbm, bo_ref, in_sem.at[2])
+    bo_copy.start()
+    lens_copy = pltpu.make_async_copy(lens_hbm, lens_ref, in_sem.at[3])
+    lens_copy.start()
 
     cache_in = [(pltpu.make_async_copy(k_hbm.at[i], k_v.at[i], k_sem.at[i]),
                  pltpu.make_async_copy(v_hbm.at[i], v_v.at[i], v_sem.at[i])) for i in range(local)]
@@ -219,6 +231,8 @@
             copy.start()
             wo_copies.append(copy)
 
+    bo_copy.wait()
+    lens_copy.wait()
     bo_v[...] = bo_ref[...].astype(F32)
     tiles = cols // LANES
     bias = jnp.concatenate([bo_v[pl.ds(me * tiles + j, 1), :] for j in range(tiles)], axis=1)
@@ -325,6 +339,7 @@
     rs_copies = {}
     ag_copies = {}
     d2d_copies = []
+    waiting = []
     out_copies = []
     todo = {part: list(offsets) for part in range(PARTS)}
 
@@ -402,8 +417,16 @@
             src_ref=at, dst_ref=at, send_sem=d2d_ssem.at[part, hop], recv_sem=d2d_rsem.at[part, hop],
             device_id=peer(mate), device_id_type=MESH)
         copy.start()
-        d2d_copies.append((copy, part, index + 1 - 2 * core, hop))
+        d2d_copies.append(copy)
+        waiting.append((copy, part, index + 1 - 2 * core, hop))
         place_out(part, index, out_sem.at[0, part, hop])
+        drain(4)
+
+    def drain(left):
+        while len(waiting) > left:
+            copy, part, other, hop = waiting.pop(0)
+            copy.wait_recv()
+            place_out(part, other, out_sem.at[1, part, hop])
 
     def own_step(part):
         for u in (0, 1):
@@ -458,15 +481,13 @@
     for s in range(lag, 2 * n_slots + 1 + lag):
         for part in range(PARTS):
             step_of(part, s - part * lag)
-    for copy, part, other, hop in d2d_copies:
-        copy.wait_recv()
-        place_out(part, other, out_sem.at[1, part, hop])
+    drain(0)
     for copies in q_copies + o_copies:
         for copy in copies:
             copy.wait_send()
     for copy in list(pair_copies.values()) + list(rs_copies.values()) + list(ag_copies.values()):
         copy.wait_send()
-    for copy, _, _, _ in d2d_copies:
+    for copy in d2d_copies:
         copy.wait_send()
     for out in out_copies:
         out.wait()
@@ -490,8 +511,6 @@
 
 def solution(mesh):
     n = mesh.shape['tp']
-    vmem = pl.BlockSpec(memory_space=pltpu.VMEM)
-    smem = pl.BlockSpec(memory_space=pltpu.SMEM)
     anywhere = pl.BlockSpec(memory_space=pl.ANY)
     dma = pltpu.SemaphoreType.DMA
 
@@ -520,8 +539,8 @@
                 jax.ShapeDtypeStruct(k_cache.shape, BF16),
                 jax.ShapeDtypeStruct(v_cache.shape, BF16),
             ),
-            in_specs=[smem, anywhere, vmem, vmem, anywhere, vmem, anywhere, vmem, anywhere, anywhere],
-            out_specs=(vmem, anywhere, anywhere),
+            in_specs=[anywhere] * 10,
+            out_specs=(anywhere, anywhere, anywhere),
             scratch_shapes=[
                 pltpu.VMEM((steps, group, width), BF16),
                 pltpu.VMEM((total, width), BF16),
@@ -536,7 +555,13 @@
                 pltpu.VMEM((1, q_cols), F32),
                 pltpu.VMEM((1, kv_cols), F32),
                 pltpu.VMEM((local * 8, kv_cols), F32),
-                dma((steps,)), dma((2,)), dma((2, local)), dma((2, local)),
+                pltpu.VMEM(piece_shape, BF16),
+                pltpu.VMEM((width // LANES, LANES), BF16),
+                pltpu.VMEM((width // LANES, LANES), BF16),
+                pltpu.VMEM((q_cols // LANES, LANES), BF16),
+                pltpu.VMEM((kv_cols // LANES, LANES), BF16),
+                pltpu.SMEM((local,), jnp.int32),
+                dma((steps,)), dma((2,)), dma((2, local)), dma((2, local)), dma((5,)), dma((PARTS,)),
             ],
             compiler_params=pltpu.CompilerParams(vmem_limit_bytes=VMEM_LIMIT),
         )(seq_lens, x_steps, by_lanes(ln_gain), by_lanes(ln_bias), w_q, by_lanes(b_q), w_kv, by_lanes(b_kv), k_cache, v_cache)
@@ -552,7 +577,7 @@
             functools.partial(group_kernel, n, steps, block),
             name='group',
             out_shape=jax.ShapeDtypeStruct((total, width), BF16),
-            in_specs=[smem, anywhere, anywhere, anywhere, anywhere, anywhere, vmem],
+            in_specs=[anywhere] * 7,
             out_specs=anywhere,
             scratch_shapes=[
                 pltpu.VMEM(piece_shape, BF16),
@@ -578,7 +603,9 @@
                 pltpu.VMEM((n_pairs, n * PACK, rows), BF16),
                 pltpu.VMEM((n_pairs, rows, n * PACK), BF16),
                 pltpu.VMEM((n_pairs, rows, n * PACK), BF16),
-                dma((2,)), dma((local,)), dma((local,)), dma((n,)),
+                pltpu.VMEM((width // LANES, LANES), BF16),
+                pltpu.SMEM((local,), jnp.int32),
+                dma((4,)), dma((local,)), dma((local,)), dma((n,)),
                 dma((PARTS, n)), dma((PARTS, n)), dma((PARTS, n)), dma((PARTS, n)),
                 dma((PARTS, chips)), dma((PARTS, chips)),
                 dma((PARTS, 2, 2 * far - 1)), dma((PARTS, 2, 2 * far - 1)),

time: 99.6 us -> 93.7 us (0.941); the launches traced: 98 us -> 93.7 us
  Pallas kernels: 97.3 us -> 93 us
    pallas_call x1, Pallas kernels: 76.5 us -> 73 us  [local_block(): pl.pallas_call(functools.partial(group_kernel, n, steps, block), name='gr...]
where the time goes in v5:
time: 93.7 us
  Pallas kernels  93 us (99%)
    pallas_call x1, Pallas kernels, local_block(): pl.pallas_call(functools.partial(group_kernel, n, steps, block), name='gr...  73 us
    pallas_call x1, Pallas kernels, local_block(): pl.pallas_call(functools.partial(local_kernel, n), name='local', out_shap...  15.3 us
    pallas_call x1, Pallas kernels, local_block(): pl.pallas_call(functools.partial(order_kernel, n), name='order', grid=(wi...  4.62 us

profile of v5, /device:TPU:21, one launch (start us, length us, event | category | flops | bytes accessed | tf_op | source)
XLA Modules:
  0.0 93.7 jit_solution(6774685477587699135)
XLA Ops:
  0.6 0.0 copy-start
  0.6 0.0 copy-start.1
  0.7 15.3 %local.1 = (bf16[2,256,256]{2,1,0:T(8,128)(2,1)}, bf16[6,3072,128]{2,1,0:T(8,128)(2,1)}, bf16[6,3072,128]{2,1,0:T(8,128)(2,1)}) custom-call(s32[6]{0:T(128)} %lens_hbm.3, bf16[3,96,6144]{2,1,0:T(8,128)(2,1)} %x_hbm.1, bf16[48,128]{1,0:T(8,128)(2,1)} %bitcast.10, bf16[48,128]{1,0:T(8,128)(2,1)} %bitcast.11, bf16[6144,384]{1,0:T(8,128)(2,1)} %wq_hbm.1, ...), custom_call_target="tpu_custom_call" | custom-call | tf_op jit(solution)/shard_map/local/pallas_call | solution.py:534
  16.0 0.0 copy-done
  16.0 0.0 copy-done.1
  16.0 73.0 %group.1 = bf16[288,6144]{1,0:T(8,128)(2,1)S(1)} custom-call(s32[6]{0:T(128)S(1)} %copy-done.1, bf16[2,256,256]{2,1,0:T(8,128)(2,1)} %get-tuple-element.6.pieces_hbm, bf16[6,3072,128]{2,1,0:T(8,128)(2,1)} %get-tuple-element.4.k_hbm, bf16[6,3072,128]{2,1,0:T(8,128)(2,1)} %get-tuple-element.5.v_hbm, bf16[288,6144]{1,0:T(8,128)(2,1)} %bitcast.9, ...), custom_call_target="tpu_custom_call" | custom-call | tf_op jit(solution)/shard_map/group/pallas_call | solution.py:576
  89.0 4.6 %order.1 = bf16[3,96,6144]{2,1,0:T(8,128)(2,1)} custom-call(bf16[2,3,48,6144]{3,2,1,0:T(8,128)(2,1)S(1)} %bitcast.7), custom_call_target="tpu_custom_call" | custom-call | tf_op jit(solution)/shard_map/order/pallas_call | solution.py:621
Async XLA Ops:
  0.6 15.4 %copy-start = (bf16[6144]{0:T(1024)(128)(2,1)S(1)}, bf16[6144]{0:T(1024)(128)(2,1)}, u32[]{:S(2)}) copy-start(bf16[6144]{0:T(1024)(128)(2,1)} %param.23) | copy-start | bytes 36868
  0.6 15.4 %copy-start.1 = (s32[6]{0:T(128)S(1)}, s32[6]{0:T(128)}, u32[]{:S(2)}) copy-start(s32[6]{0:T(128)} %lens_hbm.3) | copy-start | bytes 76

commit v6 on v5

--- a/solution.py
+++ b/solution.py
@@ -179,7 +179,7 @@
 
 def group_kernel(n, steps, block, lens_hbm, pieces_hbm, k_hbm, v_hbm, x_hbm, wo_hbm, bo_hbm, y_hbm,
                  pieces_v, q_recv, q_v, k_v, v_v, scores, heads_v, o_send, o_recv, a_v, wo_v, x_v, rest_v, bo_v,
-                 part_v, pair_send, pair_recv, rs_send, rs_recv, y_v, pack_v, q_hot, o_hot, bo_ref, lens_ref,
+                 part_v, pair_send, pair_recv, rs_send, rs_recv, y_v, pack_v, q_hot, o_hot, bo_ref, lens_ref, sorted_v, row_hot,
                  in_sem, k_sem, v_sem, wo_sem, q_ssem, q_rsem, o_ssem, o_rsem, pair_ssem, pair_rsem,
                  rs_ssem, rs_rsem, ag_ssem, ag_rsem, d2d_ssem, d2d_rsem, out_sem):
     me = lax.axis_index('tp')
@@ -255,6 +255,10 @@
         total, heads, lambda dest, r: (r // steps) * per_seq + dest * steps + r % steps, n, rows))
     fill(o_hot, unpack_hots(
         n, total, heads, lambda row: ((row // share) % n, (row % share) * steps + row // (n * share)), rows))
+
+    seq = iota((group, 1), 0)
+    row_hot[...] = one_hot(
+        group, group, ((seq % local) // share) * (n * share) + (seq // local) * share + seq % share)
 
     def exchange(part, send_buf, recv_buf, send_sem, recv_sem):
         mine = pl.ds(pl.multiple_of(me * PACK, PACK), PACK)
@@ -340,6 +344,7 @@
     ag_copies = {}
     d2d_copies = []
     waiting = []
+    halfway = set()
     out_copies = []
     todo = {part: list(offsets) for part in range(PARTS)}
 
@@ -405,9 +410,15 @@
         copy.start()
         ag_copies[part, d, slot] = copy
 
-    def place_out(part, index, sem):
-        out = pltpu.make_async_copy(
-            y_v.at[part, index], y_hbm.at[pl.ds(part * total, total), block_at(index)], sem)
+    def place_out(part, index, side, hop):
+        if (side, hop) not in halfway:
+            halfway.add((side, hop))
+            return
+        span = n * share
+        for s in range(steps):
+            src = jnp.concatenate([y_v[p, index, s * span:(s + 1) * span, :] for p in range(PARTS)], axis=0)
+            sorted_v[index, s * group:(s + 1) * group, :] = mm(row_hot[...], src).astype(BF16)
+        out = pltpu.make_async_copy(sorted_v.at[index], y_hbm.at[:, block_at(index)], out_sem.at[side, hop])
         out.start()
         out_copies.append(out)
 
@@ -419,14 +430,14 @@
         copy.start()
         d2d_copies.append(copy)
         waiting.append((copy, part, index + 1 - 2 * core, hop))
-        place_out(part, index, out_sem.at[0, part, hop])
+        place_out(part, index, 0, hop)
         drain(4)
 
     def drain(left):
         while len(waiting) > left:
             copy, part, other, hop = waiting.pop(0)
             copy.wait_recv()
-            place_out(part, other, out_sem.at[1, part, hop])
+            place_out(part, other, 1, hop)
 
     def own_step(part):
         for u in (0, 1):
@@ -493,20 +504,16 @@
         out.wait()
 
 
-def order_kernel(n, y_ref, out_ref, hot_v):
-    steps, group, _ = out_ref.shape
-    local = group // n
-    share = local // PARTS
-
-    @pl.when(pl.program_id(0) == 0)
-    def _():
-        seq = iota((group, 1), 0)
-        dev, i = seq // local, seq % local
-        hot_v[...] = one_hot(group, group, (i // share) * (n * share) + dev * share + i % share)
-
-    for s in range(steps):
-        src = jnp.concatenate([y_ref[part, s] for part in range(PARTS)], axis=0)
-        out_ref[s] = mm(hot_v[...], src).astype(BF16)
+def emit_kernel(y_hbm, out_hbm, sem):
+    pieces = 4
+    rows = y_hbm.shape[0] // pieces
+    copies = [
+        pltpu.make_async_copy(y_hbm.at[pl.ds(j * rows, rows)], out_hbm.at[pl.ds(j * rows, rows)], sem.at[j])
+        for j in range(pieces)]
+    for copy in copies:
+        copy.start()
+    for copy in copies:
+        copy.wait()
 
 
 def solution(mesh):
@@ -605,29 +612,29 @@
                 pltpu.VMEM((n_pairs, rows, n * PACK), BF16),
                 pltpu.VMEM((width // LANES, LANES), BF16),
                 pltpu.SMEM((local,), jnp.int32),
+                pltpu.VMEM((n, total, cols), BF16),
+                pltpu.VMEM((group, group), BF16),
                 dma((4,)), dma((local,)), dma((local,)), dma((n,)),
                 dma((PARTS, n)), dma((PARTS, n)), dma((PARTS, n)), dma((PARTS, n)),
                 dma((PARTS, chips)), dma((PARTS, chips)),
                 dma((PARTS, 2, 2 * far - 1)), dma((PARTS, 2, 2 * far - 1)),
                 dma((PARTS, 2, 2 * far - 1)), dma((PARTS, 2, 2 * far - 1)),
-                dma((PARTS, chips)), dma((PARTS, chips)), dma((2, PARTS, chips)),
+                dma((PARTS, chips)), dma((PARTS, chips)), dma((2, chips)),
             ],
             compiler_params=pltpu.CompilerParams(
                 collective_id=0, has_side_effects=True, vmem_limit_bytes=GROUP_LIMIT),
         )(seq_lens, in_hbm(pieces), in_hbm(k_out), in_hbm(v_out), in_hbm(x_steps.reshape(total, width)), in_hbm(w_out),
           by_lanes(b_out))
 
-        wide = 2 * cols
         y_steps = pl.pallas_call(
-            functools.partial(order_kernel, n),
-            name='order',
-            grid=(width // wide,),
-            out_shape=jax.ShapeDtypeStruct(x_steps.shape, BF16),
-            in_specs=[pl.BlockSpec((PARTS, steps, group // PARTS, wide), lambda c: (0, 0, 0, c))],
-            out_specs=pl.BlockSpec((steps, group, wide), lambda c: (0, 0, c)),
-            scratch_shapes=[pltpu.VMEM((group, group), BF16)],
+            emit_kernel,
+            name='emit',
+            out_shape=jax.ShapeDtypeStruct((total, width), BF16),
+            in_specs=[anywhere],
+            out_specs=anywhere,
+            scratch_shapes=[dma((4,))],
             compiler_params=pltpu.CompilerParams(vmem_limit_bytes=ORDER_LIMIT),
-        )(y.reshape(PARTS, steps, group // PARTS, width))
+        )(y).reshape(x_steps.shape)
         return y_steps, k_out, v_out
 
     row_spec = P(('dp', 'tp'), None, None)

time: 93.7 us -> 90.9 us (0.970)
  Pallas kernels: 93 us -> 90 us
    pallas_call x1, Pallas kernels: 4.62 us -> 1.82 us  [local_block(): pl.pallas_call(emit_kernel, name='emit', out_shape=jax.ShapeDtypeStruct((...]
where the time goes in v6:
time: 90.9 us; the launch traced here: 90.8 us
  Pallas kernels  90 us (99%)
    pallas_call x1, Pallas kernels, local_block(): pl.pallas_call(functools.partial(group_kernel, n, steps, block), name='gr...  72.8 us
    pallas_call x1, Pallas kernels, local_block(): pl.pallas_call(functools.partial(local_kernel, n), name='local', out_shap...  15.3 us
    pallas_call x1, Pallas kernels, local_block(): pl.pallas_call(emit_kernel, name='emit', out_shape=jax.ShapeDtypeStruct((...  1.82 us

profile of v6, /device:TPU:21, one launch (start us, length us, event | category | flops | bytes accessed | tf_op | source)
XLA Modules:
  0.0 90.8 jit_solution(12228307583642481459)
XLA Ops:
  0.6 0.0 copy-start
  0.6 0.0 copy-start.1
  0.7 15.3 %local.1 = (bf16[2,256,256]{2,1,0:T(8,128)(2,1)}, bf16[6,3072,128]{2,1,0:T(8,128)(2,1)}, bf16[6,3072,128]{2,1,0:T(8,128)(2,1)}) custom-call(s32[6]{0:T(128)} %lens_hbm.3, bf16[3,96,6144]{2,1,0:T(8,128)(2,1)} %x_hbm.1, bf16[48,128]{1,0:T(8,128)(2,1)} %bitcast.10, bf16[48,128]{1,0:T(8,128)(2,1)} %bitcast.11, bf16[6144,384]{1,0:T(8,128)(2,1)} %wq_hbm.1, ...), custom_call_target="tpu_custom_call" | custom-call | tf_op jit(solution)/shard_map/local/pallas_call | solution.py:541
  16.0 0.0 copy-done
  16.0 0.0 copy-done.1
  16.0 72.8 %group.1.y_hbm = bf16[288,6144]{1,0:T(8,128)(2,1)S(1)} custom-call(s32[6]{0:T(128)S(1)} %copy-done.1, bf16[2,256,256]{2,1,0:T(8,128)(2,1)} %get-tuple-element.6.pieces_hbm, bf16[6,3072,128]{2,1,0:T(8,128)(2,1)} %get-tuple-element.4.k_hbm, bf16[6,3072,128]{2,1,0:T(8,128)(2,1)} %get-tuple-element.5.v_hbm, bf16[288,6144]{1,0:T(8,128)(2,1)} %bitcast.8, ...), custom_call_target="tpu_custom_call" | custom-call | tf_op jit(solution)/shard_map/group/pallas_call | solution.py:583
  88.8 1.8 %emit.1 = bf16[288,6144]{1,0:T(8,128)(2,1)} custom-call(bf16[288,6144]{1,0:T(8,128)(2,1)S(1)} %group.1.y_hbm), custom_call_target="tpu_custom_call" | custom-call | tf_op jit(solution)/shard_map/emit/pallas_call | solution.py:629
Async XLA Ops:
  0.6 15.4 %copy-start = (bf16[6144]{0:T(1024)(128)(2,1)S(1)}, bf16[6144]{0:T(1024)(128)(2,1)}, u32[]{:S(2)}) copy-start(bf16[6144]{0:T(1024)(128)(2,1)} %param.23) | copy-start | bytes 36868
  0.6 15.4 %copy-start.1 = (s32[6]{0:T(128)S(1)}, s32[6]{0:T(128)}, u32[]{:S(2)}) copy-start(s32[6]{0:T(128)} %lens_hbm.3) | copy-start | bytes 76
